TPU v7x, 32 devices: a whole 2x2x4 slice. The times are simulated.
32 devices in a mesh: depth: 4 (over z), sample: 4 (over y, x), filter: 2 (over core).
Axes of the slice: x: 2, y: 2, z: 4, core: 2. Of those that a mesh axis runs over, the one named last changes fastest.
Arguments:
- inputs: float32 [4, 8, 8, 8, 256], P('sample', 'depth', None, None, 'filter'), may hold values from -6 to 6
- pre_gelu: float32 [4, 8, 8, 8, 256], P('sample', 'depth', None, None, 'filter'), may hold values from -6 to 6
- output_grad: float32 [4, 8, 8, 8, 256], P('sample', 'depth', None, None, 'filter'), may hold values from -6 to 6
- first_weight: float32 [27, 256, 256], P(None, None, 'filter'), may hold values from -0.078125 to 0.078125
- second_weight: float32 [27, 256, 256], P(None, None, 'filter'), may hold values from -0.078125 to 0.078125
Outputs:
- input_grad: float32 [4, 8, 8, 8, 256], P('sample', 'depth', None, None, 'filter')
- first_weight_grad: float32 [27, 256, 256], P(None, 'depth', 'filter')
- second_weight_grad: float32 [27, 256, 256], P(None, 'depth', 'filter')
All inputs are finite; a program needn't handle non-finite values.
Results may differ from a plain program's by a relative error of at most 0.000098.
Values sent between devices are 32-bit elements; how exact they have to be, the bound alone decides.
No kernel may reach another device: no remote copies, remote signals or barrier semaphores. Data moves between devices by JAX's collectives and lax.ppermute only.
A program may use at most 64 MiB of HBM per device.

v0:
```python
import math

import jax
import jax.numpy as jnp
from jax import lax
from jax.sharding import PartitionSpec as P

highest = lax.Precision.HIGHEST


def padded_2(cells, sides, width):
    for axis, dim in sides:
        count = lax.axis_size(axis)
        ends = count - 1
        head = lax.slice_in_dim(cells, 0, width, axis=dim)
        tail = lax.slice_in_dim(cells, cells.shape[dim] - width, cells.shape[dim], axis=dim)
        cells = jnp.concatenate(
            [
                lax.ppermute(tail, axis, [(i, (i + 1) % count) for i in range(ends)]),
                cells,
                lax.ppermute(head, axis, [((i + 1) % count, i) for i in range(ends)]),
            ],
            axis=dim,
        )
    return cells


def gelu_pair(pre):
    normal_cdf = 0.5 * (1.0 + lax.erf(pre * 0.7071067811865476))
    density = jnp.exp(-0.5 * pre * pre) * 0.3989422804014327
    return (pre * normal_cdf, normal_cdf + pre * density)


def pad_sides(field):
    return jnp.pad(field, [(0, 0)] * (field.ndim - 3) + [(1, 1), (1, 1), (0, 0)])


def patches(padded, flipped):
    planes = padded.shape[-4] - 2
    height = padded.shape[-3] - 2
    breadth = padded.shape[-2] - 2
    pieces = []
    for depth_tap in range(3):
        for row_tap in range(3):
            for column_tap in range(3):
                start_plane = 2 - depth_tap if flipped else depth_tap
                start_row = 2 - row_tap if flipped else row_tap
                start_column = 2 - column_tap if flipped else column_tap
                pieces.append(
                    padded[
                        ...,
                        start_plane : start_plane + planes,
                        start_row : start_row + height,
                        start_column : start_column + breadth,
                        :,
                    ]
                )
    stacked = jnp.stack(pieces, axis=-2)
    return stacked.reshape(-1, 27, padded.shape[-1])


def spread_back(grad_local, kernel):
    planes = padded_2(grad_local, (("depth", 1),), 1)
    columns = patches(pad_sides(planes), True)
    partial_value = jnp.einsum("rtc,tic->ri", columns, kernel, precision=highest)
    partial_value = partial_value.reshape(grad_local.shape[:4] + (kernel.shape[1],))
    return lax.psum_scatter(partial_value, "filter", scatter_dimension=4, tiled=True)


def reduce_weight(raw_pair):
    summed = lax.psum(raw_pair, "sample")
    return lax.psum_scatter(summed, "depth", scatter_dimension=1, tiled=True)


def local(inputs, pre_gelu, output_grad, first_weight, second_weight):
    activated, slope = gelu_pair(pre_gelu)
    stacked = jnp.stack([inputs, activated], axis=0)
    planes = padded_2(stacked, (("depth", 2),), 1)
    whole = lax.all_gather(planes, "filter", axis=5, tiled=True)
    padded = pad_sides(whole)
    local_width = output_grad.shape[4]
    act_columns = patches(padded[1], False)
    second_raw = jnp.einsum(
        "rti,rc->tic", act_columns, output_grad.reshape(-1, local_width), precision=highest
    )
    act_grad = spread_back(output_grad, second_weight)
    pre_grad = act_grad * slope
    input_grad = spread_back(pre_grad, first_weight)
    input_columns = patches(padded[0], False)
    first_raw = jnp.einsum(
        "rti,rc->tic", input_columns, pre_grad.reshape(-1, local_width), precision=highest
    )
    first_sum, second_sum = reduce_weight((first_raw, second_raw))
    cells = (
        inputs.shape[0]
        * lax.axis_size("sample")
        * inputs.shape[1]
        * lax.axis_size("depth")
        * inputs.shape[2]
        * inputs.shape[3]
    )
    factor = 1.0 / math.sqrt(cells)
    return (input_grad, first_sum * factor, second_sum * factor)


def solution(mesh):
    return jax.shard_map(
        local,
        mesh=mesh,
        in_specs=(
            P("sample", "depth", None, None, "filter"),
            P("sample", "depth", None, None, "filter"),
            P("sample", "depth", None, None, "filter"),
            P(None, None, "filter"),
            P(None, None, "filter"),
        ),
        out_specs=(
            P("sample", "depth", None, None, "filter"),
            P(None, "depth", "filter"),
            P(None, "depth", "filter"),
        ),
        check_vma=False,
    )
```

profile of v0, /device:TPU:0, one launch (start us, length us, event | category | flops | bytes accessed | tf_op | source)
XLA Modules:
  0.0 276.8 jit_solution(6035970452476575996)
XLA Ops:
  7.2 0.9 fusion.34
  8.2 1.4 collective-permute-start.1
  9.6 5.6 %collective-permute-start = (f32[1,1,8,8,128]{4,3,2,1,0:T(8,128)S(1)}, f32[1,1,8,8,128]{4,3,2,1,0:T(8,128)S(1)}, u32[]{:S(2)}, u32[]{:S(2)}) collective-permute-start(f32[1,1,8,8,128]{4,3,2,1,0:T(8,128)S(1)} %get-tuple-element.65), channel_id=1, source_target_pairs={{0,8},{8,16},{16,24},{1,9},{9,17},{17,25},{2,10},{10,18},{18,26},{... | collective-permute-start | bytes 98312 | tf_op jit(solution)/shard_map/ppermute | solution.py:19
  15.2 1.6 collective-permute-done
  18.3 3.4 %fusion.2 = f32[2,8,8,256,1]{3,2,0,1,4:T(8,128)S(1)} fusion(f32[27,256,128]{2,1,0:T(8,128)S(1)} %copy-done, f32[2,8,8,128,27]{3,2,1,0,4:T(8,128)S(1)} %bitcast.339), kind=kOutput, calls=%fused_computation.2 | convolution fusion | flops 1358954496 | bytes 5439488 | tf_op jit(solution)/shard_map/rtc,tic->ri/dot_general | solution.py:65
  22.4 10.1 %reduce-scatter.5.cloned.1.call-done = f32[1,2,8,8,128]{4,3,2,1,0:T(8,128)} async-done(((f32[1,2,8,8,256]{4,3,2,1,0:T(8,128)}), f32[1,2,8,8,128]{4,3,2,1,0:T(8,128)}) %reduce-scatter.5.cloned.1.call-update) | async-done | bytes 65552 | tf_op jit(solution)/shard_map/reduce_scatter | solution.py:67
  34.2 1.3 collective-permute-start.5
  35.5 4.5 %collective-permute-start.4 = (f32[2,1,1,8,8,128]{5,4,3,2,1,0:T(8,128)S(1)}, f32[2,1,1,8,8,128]{5,4,3,2,1,0:T(8,128)S(1)}, u32[]{:S(2)}, u32[]{:S(2)}) collective-permute-start(f32[2,1,1,8,8,128]{5,4,3,2,1,0:T(8,128)S(1)} %get-tuple-element.55), channel_id=1, source_target_pairs={{0,8},{8,16},{16,24},{1,9},{9,17},{17,25},{2,10},{10,18},{18,26},{... | collective-permute-start | bytes 196616 | tf_op jit(solution)/shard_map/ppermute | solution.py:19
  40.4 1.5 collective-permute-done.4
  42.8 2.2 all_gather.3
  45.0 1.0 fusion.17
  46.6 7.7 %fusion.8 = f32[27,256,128]{2,1,0:T(8,128)} fusion(f32[1,2,8,8,27,256]{5,3,2,1,4,0:T(8,128)S(1)} %constant_dynamic-update-slice_fusion.54, f32[1,2,8,8,128]{4,3,2,1,0:T(8,128)S(1)} %get-tuple-element.58), kind=kOutput, calls=%fused_computation.8 | convolution fusion | flops 1358954496 | bytes 7143424 | tf_op jit(solution)/shard_map/rti,rc->tic/dot_general | solution.py:90
  54.6 1.0 constant_dynamic-update-slice_fusion.107
  55.6 1.0 constant_dynamic-update-slice_fusion.106
  56.6 1.0 constant_dynamic-update-slice_fusion.105
  57.5 0.9 constant_dynamic-update-slice_fusion.104
  58.5 1.0 constant_dynamic-update-slice_fusion.103
  59.4 1.0 constant_dynamic-update-slice_fusion.102
  61.3 1.0 constant_dynamic-update-slice_fusion.100
  62.3 1.0 constant_dynamic-update-slice_fusion.99
  64.3 1.0 constant_dynamic-update-slice_fusion.97
  65.3 1.0 constant_dynamic-update-slice_fusion.96
  67.2 1.0 constant_dynamic-update-slice_fusion.94
  68.5 7.7 %fusion.11 = f32[27,256,128]{2,1,0:T(8,128)} fusion(f32[1,2,8,8,27,256]{5,3,2,1,4,0:T(8,128)S(1)} %constant_dynamic-update-slice_fusion.81, f32[1,2,8,8,128]{4,3,2,1,0:T(8,128)S(1)} %copy-done.5), kind=kOutput, calls=%fused_computation.9 | convolution fusion | flops 1358954496 | bytes 7143424 | tf_op jit(solution)/shard_map/rti,rc->tic/dot_general | solution.py:83
  77.2 1.3 collective-permute-start.3
  78.4 4.9 %collective-permute-start.2 = (f32[1,1,8,8,128]{4,3,2,1,0:T(8,128)S(1)}, f32[1,1,8,8,128]{4,3,2,1,0:T(8,128)S(1)}, u32[]{:S(2)}, u32[]{:S(2)}) collective-permute-start(f32[1,1,8,8,128]{4,3,2,1,0:T(8,128)S(1)} %get-tuple-element.61), channel_id=1, source_target_pairs={{0,8},{8,16},{16,24},{1,9},{9,17},{17,25},{2,10},{10,18},{18,26},{... | collective-permute-start | bytes 98312 | tf_op jit(solution)/shard_map/ppermute | solution.py:19
  83.3 1.3 collective-permute-done.3
  84.6 0.9 collective-permute-done.2
  89.0 1.4 pad_maximum_fusion.2
  97.6 26.0 %reduce-scatter.9.cloned.1.call-done = f32[27,64,128]{2,1,0:T(8,128)} async-done(((f32[27,256,128]{2,1,0:T(8,128)}), f32[27,64,128]{2,1,0:T(8,128)}) %reduce-scatter.9.cloned.1.call-update) | async-done | bytes 884752 | tf_op jit(solution)/shard_map/reduce_scatter | solution.py:72
  123.7 69.1 %reduce-scatter.11.cloned.1.call-done = f32[27,64,128]{2,1,0:T(8,128)} async-done(((f32[27,256,128]{2,1,0:T(8,128)}), f32[27,64,128]{2,1,0:T(8,128)}) %reduce-scatter.11.cloned.1.call-update) | async-done | bytes 884752 | tf_op jit(solution)/shard_map/reduce_scatter | solution.py:72
  192.8 1.5 constant_dynamic-update-slice_fusion.39
  194.3 1.5 constant_dynamic-update-slice_fusion.38
  195.7 1.5 constant_dynamic-update-slice_fusion.37
  197.2 1.5 constant_dynamic-update-slice_fusion.36
  198.7 1.5 constant_dynamic-update-slice_fusion.35
  200.1 1.5 constant_dynamic-update-slice_fusion.34
  201.6 1.5 constant_dynamic-update-slice_fusion.33
  203.1 1.5 constant_dynamic-update-slice_fusion.32
  204.5 1.5 constant_dynamic-update-slice_fusion.31
  206.0 1.5 constant_dynamic-update-slice_fusion.30
  207.5 1.5 constant_dynamic-update-slice_fusion.29
  209.0 1.5 constant_dynamic-update-slice_fusion.28
  210.4 1.5 constant_dynamic-update-slice_fusion.27
  211.9 5.9 %fusion = f32[2,8,8,256,1]{3,2,0,1,4:T(8,128)S(1)} fusion(f32[27,256,128]{2,1,0:T(8,128)} %param.8, f32[2,8,8,128,27]{3,2,1,0,4:T(8,128)} %bitcast.61), kind=kOutput, calls=%fused_computation | convolution fusion | flops 1358954496 | bytes 5439488 | tf_op jit(solution)/shard_map/rtc,tic->ri/dot_general | solution.py:65
  218.5 41.5 %all-reduce.6.cloned.1.call-done = (f32[27,64,128]{2,1,0:T(8,128)}, f32[27,64,128]{2,1,0:T(8,128)}) async-done(((f32[27,64,128]{2,1,0:T(8,128)}, f32[27,64,128]{2,1,0:T(8,128)}), (f32[27,64,128]{2,1,0:T(8,128)}, f32[27,64,128]{2,1,0:T(8,128)})) %all-reduce.6.cloned.1.call-update) | async-done | bytes 1769488 | tf_op jit(solution)/shard_map/psum | solution.py:71
  260.0 2.9 %broadcast_multiply_fusion = (f32[27,64,128]{2,1,0:T(8,128)}, f32[27,64,128]{2,1,0:T(8,128)}) fusion(f32[27,64,128]{2,1,0:T(8,128)} %get-tuple-element.4, f32[27,64,128]{2,1,0:T(8,128)} %get-tuple-element.3), kind=kLoop, calls=%fused_computation.20 | loop fusion | flops 442368 | bytes 3538944 | tf_op jit(solution)/shard_map/mul | solution.py:103
  262.9 7.3 %reduce-scatter.7.cloned.1.call-done = f32[1,2,8,8,128]{4,3,2,1,0:T(8,128)} async-done(((f32[1,2,8,8,256]{4,3,2,1,0:T(8,128)}), f32[1,2,8,8,128]{4,3,2,1,0:T(8,128)}) %reduce-scatter.7.cloned.1.call-update) | async-done | bytes 65552 | tf_op jit(solution)/shard_map/reduce_scatter | solution.py:67
  (121 shorter events, 20.8 us)
Async XLA Ops:
  7.2 11.1 %copy-start = (f32[27,256,128]{2,1,0:T(8,128)S(1)}, f32[27,256,128]{2,1,0:T(8,128)}, u32[]{:S(2)}) copy-start(f32[27,256,128]{2,1,0:T(8,128)} %param.9) | copy-start | bytes 10616836
  7.2 25.3 %reduce-scatter.5.cloned.1.call-start = ((), (), s32[]{:S(2)}) async-start(), calls=%async_computation.4 | async-start | bytes 196608 | tf_op jit(solution)/shard_map/reduce_scatter | solution.py:67
  7.2 10.6 %copy-start.4 = (f32[1,2,8,8,128]{4,3,2,1,0:T(8,128)S(1)}, f32[1,2,8,8,128]{4,3,2,1,0:T(8,128)}, u32[]{:S(2)}) copy-start(f32[1,2,8,8,128]{4,3,2,1,0:T(8,128)} %param.7) | copy-start | bytes 196612
  8.2 7.0 %collective-permute-start.1 = (f32[1,1,8,8,128]{4,3,2,1,0:T(8,128)S(1)}, f32[1,1,8,8,128]{4,3,2,1,0:T(8,128)S(1)}, u32[]{:S(2)}, u32[]{:S(2)}) collective-permute-start(f32[1,1,8,8,128]{4,3,2,1,0:T(8,128)S(1)} %get-tuple-element.66), channel_id=1, source_target_pairs={{8,0},{16,8},{24,16},{9,1},{17,9},{25,17},{10,2},{18,10},{26,18},{... | collective-permute-start | bytes 98312 | tf_op jit(solution)/shard_map/ppermute | solution.py:21
  9.6 7.2 %collective-permute-start = (f32[1,1,8,8,128]{4,3,2,1,0:T(8,128)S(1)}, f32[1,1,8,8,128]{4,3,2,1,0:T(8,128)S(1)}, u32[]{:S(2)}, u32[]{:S(2)}) collective-permute-start(f32[1,1,8,8,128]{4,3,2,1,0:T(8,128)S(1)} %get-tuple-element.65), channel_id=1, source_target_pairs={{0,8},{8,16},{16,24},{1,9},{9,17},{17,25},{2,10},{10,18},{18,26},{... | collective-permute-start | bytes 98312 | tf_op jit(solution)/shard_map/ppermute | solution.py:19
  22.3 101.4 %reduce-scatter.9.cloned.1.call-start = ((), (), s32[]{:S(2)}) async-start(), calls=%async_computation.6 | async-start | bytes 4423680 | tf_op jit(solution)/shard_map/reduce_scatter | solution.py:72
  33.4 13.2 %copy-start.2 = (f32[1,2,8,8,128]{4,3,2,1,0:T(8,128)}, f32[1,2,8,8,128]{4,3,2,1,0:T(8,128)S(1)}, u32[]{:S(2)}) copy-start(f32[1,2,8,8,128]{4,3,2,1,0:T(8,128)S(1)} %get-tuple-element.58) | copy-start | bytes 196612
  34.2 6.2 %collective-permute-start.5 = (f32[2,1,1,8,8,128]{5,4,3,2,1,0:T(8,128)S(1)}, f32[2,1,1,8,8,128]{5,4,3,2,1,0:T(8,128)S(1)}, u32[]{:S(2)}, u32[]{:S(2)}) collective-permute-start(f32[2,1,1,8,8,128]{5,4,3,2,1,0:T(8,128)S(1)} %get-tuple-element.56), channel_id=1, source_target_pairs={{8,0},{16,8},{24,16},{9,1},{17,9},{25,17},{10,2},{18,10},{26,18},{... | collective-permute-start | bytes 196616 | tf_op jit(solution)/shard_map/ppermute | solution.py:21
  35.5 6.4 %collective-permute-start.4 = (f32[2,1,1,8,8,128]{5,4,3,2,1,0:T(8,128)S(1)}, f32[2,1,1,8,8,128]{5,4,3,2,1,0:T(8,128)S(1)}, u32[]{:S(2)}, u32[]{:S(2)}) collective-permute-start(f32[2,1,1,8,8,128]{5,4,3,2,1,0:T(8,128)S(1)} %get-tuple-element.55), channel_id=1, source_target_pairs={{0,8},{8,16},{16,24},{1,9},{9,17},{17,25},{2,10},{10,18},{18,26},{... | collective-permute-start | bytes 196616 | tf_op jit(solution)/shard_map/ppermute | solution.py:19
  54.3 138.4 %reduce-scatter.11.cloned.1.call-start = ((), (), s32[]{:S(2)}) async-start(), calls=%async_computation.7 | async-start | bytes 4423680 | tf_op jit(solution)/shard_map/reduce_scatter | solution.py:72
  54.6 13.6 %copy-start.1 = (f32[1,4,10,10,256]{4,3,2,1,0:T(8,128)S(1)}, f32[1,4,10,10,256]{4,3,2,1,0:T(8,128)}, u32[]{:S(2)}) copy-start(f32[1,4,10,10,256]{4,3,2,1,0:T(8,128)} %get-tuple-element.5) | copy-start | bytes 1228804
  54.6 13.9 %copy-start.5 = (f32[1,2,8,8,128]{4,3,2,1,0:T(8,128)S(1)}, f32[1,2,8,8,128]{4,3,2,1,0:T(8,128)}, u32[]{:S(2)}) copy-start(f32[1,2,8,8,128]{4,3,2,1,0:T(8,128)} %param.7) | copy-start | bytes 196612
  76.3 183.7 %all-reduce.6.cloned.1.call-start = ((), (), s32[]{:S(2)}) async-start(), calls=%async_computation.8 | async-start | bytes 3538944 | tf_op jit(solution)/shard_map/psum | solution.py:71
  76.3 20.7 %copy-start.3 = (f32[1,2,8,8,128]{4,3,2,1,0:T(8,128)S(1)}, f32[1,2,8,8,128]{4,3,2,1,0:T(8,128)}, u32[]{:S(2)}) copy-start(f32[1,2,8,8,128]{4,3,2,1,0:T(8,128)} %copy-done.2) | copy-start | bytes 196612
  77.2 7.5 %collective-permute-start.3 = (f32[1,1,8,8,128]{4,3,2,1,0:T(8,128)S(1)}, f32[1,1,8,8,128]{4,3,2,1,0:T(8,128)S(1)}, u32[]{:S(2)}, u32[]{:S(2)}) collective-permute-start(f32[1,1,8,8,128]{4,3,2,1,0:T(8,128)S(1)} %get-tuple-element.62), channel_id=1, source_target_pairs={{8,0},{16,8},{24,16},{9,1},{17,9},{25,17},{10,2},{18,10},{26,18},{... | collective-permute-start | bytes 98312 | tf_op jit(solution)/shard_map/ppermute | solution.py:21
  78.4 7.1 %collective-permute-start.2 = (f32[1,1,8,8,128]{4,3,2,1,0:T(8,128)S(1)}, f32[1,1,8,8,128]{4,3,2,1,0:T(8,128)S(1)}, u32[]{:S(2)}, u32[]{:S(2)}) collective-permute-start(f32[1,1,8,8,128]{4,3,2,1,0:T(8,128)S(1)} %get-tuple-element.61), channel_id=1, source_target_pairs={{0,8},{8,16},{16,24},{1,9},{9,17},{17,25},{2,10},{10,18},{18,26},{... | collective-permute-start | bytes 98312 | tf_op jit(solution)/shard_map/ppermute | solution.py:19
  192.7 77.5 %reduce-scatter.7.cloned.1.call-start = ((), (), s32[]{:S(2)}) async-start(), calls=%async_computation.5 | async-start | bytes 196608 | tf_op jit(solution)/shard_map/reduce_scatter | solution.py:67
Sparse Core Ops, SparseCore 0:
  22.4 9.9 reduce-scatter.4
  54.5 69.1 reduce-scatter.8
  126.0 66.6 reduce-scatter.10
  195.8 64.1 all-reduce.5
  262.6 7.5 reduce-scatter.6
where the time goes:
time: 278 us; the launch traced here: 277 us
  waiting for transfers between devices  160 us (58%)
  local copies, waits for them, and re-layouts  47.5 us (17%)
  matrix products  24.7 us (9%)
  starting transfers between devices  19.4 us (7%)
  between operations  14.6 us (5%)
  other arithmetic  8.71 us (3%)
    reduce_scatter x2, waiting for transfers between devices, reduce_weight(): return lax.psum_scatter(summed, 'depth', scatter_dimension=1, tiled=True)  95.1 us
    psum x1, waiting for transfers between devices, reduce_weight(): summed = lax.psum(raw_pair, 'sample')  41.5 us
    unnamed x116, local copies, waits for them, and re-layouts  40.8 us
    reduce_scatter x2, waiting for transfers between devices, spread_back(): lax.psum_scatter(partial_value, 'filter', scatter_dimension=4, tiled=True)  17.4 us
    ppermute x3, starting transfers between devices, padded_2(): lax.ppermute(tail, axis, [(i, (i + 1) % count) for i in range(ends)])  15 us
    dot_general x2, matrix products, spread_back(): jnp.einsum('rtc,tic->ri', columns, kernel, precision=highest)  9.26 us
    dot_general x1, matrix products, local(): jnp.einsum('rti,rc->tic', act_columns, output_grad.reshape(-1, local_widt...  7.74 us
    dot_general x1, matrix products, local(): jnp.einsum('rti,rc->tic', input_columns, pre_grad.reshape(-1, local_width...  7.71 us
  transfers between devices with their start and end apart: 11, of which 10 were waited for; matrix products, arithmetic and copies ran while one was open for 23% of the time, Pallas kernels for 0%

commit v1 on v0

--- a/solution.py
+++ b/solution.py
@@ -1,8 +1,11 @@
+import functools
 import math
 
 import jax
 import jax.numpy as jnp
 from jax import lax
+from jax.experimental import pallas as pl
+from jax.experimental.pallas import tpu as pltpu
 from jax.sharding import PartitionSpec as P
 
 highest = lax.Precision.HIGHEST
@@ -72,7 +75,385 @@
     return lax.psum_scatter(summed, "depth", scatter_dimension=1, tiled=True)
 
 
+def axis_sizes():
+    return lax.axis_size("depth"), lax.axis_size("sample"), lax.axis_size("filter")
+
+
+def gather_plan_fits(inputs, output_grad, second_weight):
+    depths, samples, halves = axis_sizes()
+    batch, planes, height, breadth, lanes = output_grad.shape
+    rows = batch * samples * planes * depths * height * breadth
+    return (
+        batch == 1
+        and halves == 2
+        and lanes == 128
+        and breadth == 8
+        and height % 2 == 0
+        and second_weight.shape[1] == halves * lanes
+        and 2 * second_weight.shape[1] == depths * lanes
+        and samples & (samples - 1) == 0
+        and rows * lanes * 4 <= 2**21
+    )
+
+
+def column_shift(cells, tap):
+    if tap == 1:
+        return cells
+    breadth = cells.shape[1]
+    rolled = pltpu.roll(cells, 1 if tap == 0 else breadth - 1, axis=1)
+    column = lax.broadcasted_iota(jnp.int32, cells.shape, 1)
+    return jnp.where(column == (0 if tap == 0 else breadth - 1), 0.0, rolled)
+
+
+def two_parts(cells):
+    high = cells.astype(jnp.bfloat16)
+    return high, (cells - high.astype(jnp.float32)).astype(jnp.bfloat16)
+
+
+def row_pairs(cells):
+    height, breadth, lanes = cells.shape
+    edge = jnp.zeros((1, breadth, lanes), jnp.float32)
+    even = jnp.concatenate([edge, cells, edge], axis=0)
+    even = even.reshape(height // 2 + 1, 2 * breadth, lanes)
+    return even, cells.reshape(height // 2, 2 * breadth, lanes)
+
+
+def spread_field(get_plane, planes, even_ref, odd_ref):
+    for plane in range(planes):
+        source = get_plane(plane)
+        for tap in range(3):
+            even, odd = row_pairs(column_shift(source, tap))
+            for part, value in enumerate(two_parts(even)):
+                even_ref[tap, part, plane] = value
+            for part, value in enumerate(two_parts(odd)):
+                odd_ref[tap, part, plane] = value
+
+
+def slab(even_ref, odd_ref, lead, first, planes, row_tap):
+    pairs = odd_ref.shape[-3]
+    where = pl.ds(first, planes)
+    if row_tap == 1:
+        value = odd_ref[(*lead, where)]
+    else:
+        start = row_tap // 2
+        value = even_ref[(*lead, where, slice(start, start + pairs))]
+    return value.reshape(-1, value.shape[-1])
+
+
+def back_step(first, planes, weight_ref, even_ref, odd_ref, cells_first):
+    height = weight_ref.shape[1]
+    total = None
+    for row_tap in range(3):
+        left = []
+        right = []
+        for column_tap in range(3):
+            kernel_high, kernel_low = two_parts(weight_ref[3 * row_tap + column_tap])
+            cell = [
+                slab(even_ref, odd_ref, (2 - column_tap, part), first, planes, 2 - row_tap)
+                for part in range(2)
+            ]
+            left += [cell[0], cell[1], cell[0]]
+            right += [kernel_high, kernel_high, kernel_low]
+        left = jnp.concatenate(left, axis=1)
+        right = jnp.concatenate(right, axis=1)
+        if not cells_first:
+            left, right = right, left
+        product = lax.dot_general(
+            left, right, (((1,), (1,)), ((), ())), preferred_element_type=jnp.float32
+        )
+        total = product if total is None else total + product
+    return total
+
+
+def split_halves(total, keep_ref, send_ref):
+    width = keep_ref.shape[-1]
+    mine = lax.axis_index("filter") == 0
+    low, high = total[:, :width], total[:, width:]
+    keep_ref[...] = jnp.where(mine, low, high)
+    send_ref[...] = jnp.where(mine, high, low)
+
+
+def act_back_kernel(field_ref, weight_ref, keep_ref, send_ref, even_ref, odd_ref, total_ref):
+    step = pl.program_id(0)
+    planes = field_ref.shape[0]
+
+    @pl.when(step == 0)
+    def _():
+        for ref in (even_ref, odd_ref):
+            for tap in range(3):
+                for part in range(2):
+                    for plane in (0, planes + 1):
+                        ref[tap, part, plane] = jnp.zeros(ref.shape[3:], ref.dtype)
+        spread_field(
+            lambda plane: field_ref[plane],
+            planes,
+            even_ref.at[:, :, 1 : planes + 1],
+            odd_ref.at[:, :, 1 : planes + 1],
+        )
+        total_ref[...] = jnp.zeros_like(total_ref)
+
+    total_ref[...] += back_step(2 - step, planes, weight_ref, even_ref, odd_ref, True)
+
+    @pl.when(step == 2)
+    def _():
+        split_halves(total_ref[...], keep_ref, send_ref)
+
+
+def input_back_kernel(planes, field_ref, weight_ref, keep_ref, send_ref, even_ref, odd_ref, total_ref):
+    step = pl.program_id(0)
+    depths = field_ref.shape[0]
+
+    @pl.when(step == 0)
+    def _():
+        first = lax.axis_index("depth") * planes
+
+        def plane_at(offset):
+            place = first + offset - 1
+            inside = (place >= 0) & (place < depths)
+            return jnp.where(inside, field_ref[jnp.clip(place, 0, depths - 1)], 0.0)
+
+        spread_field(plane_at, planes + 2, even_ref, odd_ref)
+        total_ref[...] = jnp.zeros_like(total_ref)
+
+    total_ref[...] += back_step(2 - step, planes, weight_ref, even_ref, odd_ref, False)
+
+    @pl.when(step == 2)
+    def _():
+        split_halves(total_ref[...].T, keep_ref, send_ref)
+
+
+def full_spec(shape):
+    return pl.BlockSpec(shape, lambda *_: (0,) * len(shape))
+
+
+def spread_scratch(planes, height, breadth, lanes, parts):
+    return [
+        pltpu.VMEM((3, parts, planes, height // 2 + 1, 2 * breadth, lanes), jnp.bfloat16),
+        pltpu.VMEM((3, parts, planes, height // 2, 2 * breadth, lanes), jnp.bfloat16),
+    ]
+
+
+def spread_call(field, kernel, planes, whole):
+    depths, height, breadth, lanes = field.shape
+    taps, ins, outs = kernel.shape
+    rows = planes * height * breadth
+    body = act_back_kernel if whole else functools.partial(input_back_kernel, planes)
+    return pl.pallas_call(
+        body,
+        grid=(3,),
+        in_specs=[
+            full_spec(field.shape),
+            pl.BlockSpec((taps // 3, ins, outs), lambda step: (step, 0, 0)),
+        ],
+        out_specs=[full_spec((rows, ins // 2))] * 2,
+        out_shape=[jax.ShapeDtypeStruct((rows, ins // 2), jnp.float32)] * 2,
+        scratch_shapes=spread_scratch(planes + 2, height, breadth, lanes, 2)
+        + [pltpu.VMEM((rows, ins) if whole else (ins, rows), jnp.float32)],
+        compiler_params=pltpu.CompilerParams(vmem_limit_bytes=48 * 2**20),
+        cost_estimate=pl.CostEstimate(
+            flops=6 * rows * taps * ins * outs, transcendentals=0, bytes_accessed=4 * kernel.size
+        ),
+        name="act_back" if whole else "input_back",
+    )(field, kernel)
+
+
+def join_kernel(*refs):
+    *pieces, out_ref = refs
+    count = len(pieces)
+    planes = pieces[0].shape[0]
+    place = lax.axis_index("depth")
+    for step, piece in enumerate(pieces):
+        source = lax.rem(place + count - step, count)
+        out_ref[pl.ds(source * planes, planes)] = piece[...]
+
+
+def join_depth(pieces):
+    planes, *rest = pieces[0].shape
+    return pl.pallas_call(
+        join_kernel,
+        out_shape=jax.ShapeDtypeStruct((planes * len(pieces), *rest), jnp.float32),
+        name="join_depth",
+    )(*pieces)
+
+
+def activation_kernel(count, *refs):
+    saved, before = refs[:count], refs[count : 2 * count]
+    slope_ref, pair_ref = refs[2 * count :]
+    planes = saved[0].shape[0]
+    place = lax.axis_index("depth")
+    lower = lax.rem(place, 2) == 0
+    half = saved[0].shape[-1] // 2
+    for step in range(count):
+        source = lax.rem(place + count - step, count)
+        where = pl.ds(source * planes, planes)
+        shape = saved[step].shape
+        first = saved[step][...].reshape(-1, shape[-1])
+        activated, slope = gelu_pair(before[step][...].reshape(-1, shape[-1]))
+        slope_ref[where] = slope.reshape(shape)
+        lane = lax.broadcasted_iota(jnp.int32, first.shape, 1)
+        low = jnp.where(lane < half, first, pltpu.roll(activated, half, axis=1))
+        high = jnp.where(lane < half, pltpu.roll(first, half, axis=1), activated)
+        pair_ref[where] = jnp.where(lower, low, high).reshape(shape)
+
+
+def activation_call(saved, before):
+    planes, *rest = saved[0].shape
+    count = len(saved)
+    shape = (planes * count, *rest)
+    return pl.pallas_call(
+        functools.partial(activation_kernel, count),
+        out_shape=[jax.ShapeDtypeStruct(shape, jnp.float32)] * 2,
+        name="activation",
+    )(*saved, *before)
+
+
+def weight_kernel(count, second, factor, *refs):
+    fields, near, far = refs[:count], refs[count : 2 * count], refs[2 * count : 3 * count]
+    out_ref, even_ref, odd_ref, grad_ref = refs[3 * count :]
+    step = pl.program_id(0)
+    planes, height, breadth, lanes = near[0].shape
+    half = lanes // 2
+    rows = planes * height * breadth
+
+    @pl.when(step == 0)
+    def _():
+        owner = lax.axis_index("depth") // 2 == lax.axis_index("filter")
+        for sample in range(count):
+            for ref in (even_ref, odd_ref):
+                for tap in range(3):
+                    for plane in (0, planes + 1):
+                        ref[tap, sample, plane] = jnp.zeros(ref.shape[3:], ref.dtype)
+            for plane in range(planes):
+                cells = jnp.where(owner, near[sample][plane], far[sample][plane])
+                lane = lax.broadcasted_iota(jnp.int32, cells.shape, 2)
+                swapped = pltpu.roll(cells, half, axis=2)
+                lower = lane < half
+                cells = jnp.where(lower, swapped, cells) if second else jnp.where(lower, cells, swapped)
+                high = cells.astype(jnp.bfloat16).astype(jnp.float32)
+                cells = jnp.where(lower, high, cells - high)
+                for tap in range(3):
+                    even, odd = row_pairs(column_shift(cells, tap))
+                    even_ref[tap, sample, plane + 1] = even.astype(jnp.bfloat16)
+                    odd_ref[tap, sample, plane + 1] = odd.astype(jnp.bfloat16)
+            turned = fields[sample][...].reshape(rows, lanes).T
+            for part, value in enumerate(two_parts(turned)):
+                grad_ref[part * lanes : (part + 1) * lanes, sample * rows : (sample + 1) * rows] = value
+
+    def cell(row_tap, column_tap):
+        return jnp.concatenate(
+            [
+                slab(even_ref, odd_ref, (column_tap, sample), step, planes, row_tap)
+                for sample in range(count)
+            ],
+            axis=0,
+        )
+
+    taps = [(row_tap, column_tap) for row_tap in range(3) for column_tap in range(3)]
+    for start in range(0, 9, 2):
+        group = taps[start : start + 2]
+        right = [cell(*tap) for tap in group]
+        right = jnp.concatenate(right, axis=1) if len(right) > 1 else right[0]
+        product = jnp.dot(grad_ref[...], right, preferred_element_type=jnp.float32)
+        product = product[:lanes] + product[lanes:]
+        for index in range(len(group)):
+            piece = product[:, index * lanes : (index + 1) * lanes]
+            piece = piece + pltpu.roll(piece, half, axis=1)
+            out_ref[start + index] = piece.T[:half] * factor
+
+
+def weight_call(fields, near, far, second, factor):
+    planes, height, breadth, lanes = near[0].shape
+    count = len(fields)
+    rows = planes * height * breadth
+    scratch = [
+        pltpu.VMEM((3, count, planes + 2, height // 2 + 1, 2 * breadth, lanes), jnp.bfloat16),
+        pltpu.VMEM((3, count, planes + 2, height // 2, 2 * breadth, lanes), jnp.bfloat16),
+        pltpu.VMEM((2 * lanes, count * rows), jnp.bfloat16),
+    ]
+    return pl.pallas_call(
+        functools.partial(weight_kernel, count, second, factor),
+        grid=(3,),
+        in_specs=[full_spec(near[0].shape)] * (3 * count),
+        out_specs=pl.BlockSpec((9, lanes // 2, lanes), lambda step: (step, 0, 0)),
+        out_shape=jax.ShapeDtypeStruct((27, lanes // 2, lanes), jnp.float32),
+        scratch_shapes=scratch,
+        compiler_params=pltpu.CompilerParams(vmem_limit_bytes=56 * 2**20),
+        cost_estimate=pl.CostEstimate(
+            flops=4 * 2 * 27 * count * rows * lanes * lanes // 2,
+            transcendentals=0,
+            bytes_accessed=4 * 4 * count * rows * lanes,
+        ),
+        name="second_weight" if second else "first_weight",
+    )(*fields, *near, *far)
+
+
+def around_depth(field):
+    count = lax.axis_size("depth")
+    steps = [1, count - 1] + list(range(2, count - 1))
+    moved = {
+        step: lax.ppermute(field, "depth", [(i, (i + step) % count) for i in range(count)])
+        for step in steps
+    }
+    return [field] + [moved[step] for step in range(1, count)]
+
+
+def across_samples(field):
+    count = lax.axis_size("sample")
+    return [field] + [
+        lax.ppermute(field, "sample", [(i, i ^ step) for i in range(count)])
+        for step in range(1, count)
+    ]
+
+
+def owners_across_samples(pair):
+    depths, samples, halves = axis_sizes()
+    moved = [pair]
+    for step in range(1, samples):
+        links = []
+        for depth in range(depths):
+            for sample in range(samples):
+                half = depth // 2
+                place = lambda value: (depth * samples + value) * halves + half
+                links.append((place(sample), place(sample ^ step)))
+        moved.append(lax.ppermute(pair, ("depth", "sample", "filter"), links))
+    return moved
+
+
+def swap_filter(field):
+    return lax.ppermute(field, "filter", [(0, 1), (1, 0)])
+
+
+def gather_plan(inputs, pre_gelu, output_grad, first_weight, second_weight, factor):
+    local_shape = output_grad.shape
+    planes = local_shape[1]
+    inputs, pre_gelu, output_grad = inputs[0], pre_gelu[0], output_grad[0]
+    grads = join_depth(around_depth(output_grad))
+    slope, pair = activation_call(around_depth(inputs), around_depth(pre_gelu))
+    keep, send = spread_call(grads, second_weight, grads.shape[0], True)
+    pre_grad = (keep + swap_filter(send)).reshape(slope.shape) * slope
+    all_grads = across_samples(grads)
+    near = owners_across_samples(pair)
+    far = [swap_filter(piece) for piece in near]
+    all_pre = across_samples(pre_grad)
+    keep, send = spread_call(pre_grad, first_weight, planes, False)
+    input_grad = (keep + swap_filter(send)).reshape(local_shape)
+    second = weight_call(all_grads, near, far, True, factor)
+    first = weight_call(all_pre, near, far, False, factor)
+    return input_grad, first, second
+
+
 def local(inputs, pre_gelu, output_grad, first_weight, second_weight):
+    cells = (
+        inputs.shape[0]
+        * lax.axis_size("sample")
+        * inputs.shape[1]
+        * lax.axis_size("depth")
+        * inputs.shape[2]
+        * inputs.shape[3]
+    )
+    factor = 1.0 / math.sqrt(cells)
+    if gather_plan_fits(inputs, output_grad, second_weight):
+        return gather_plan(inputs, pre_gelu, output_grad, first_weight, second_weight, factor)
     activated, slope = gelu_pair(pre_gelu)
     stacked = jnp.stack([inputs, activated], axis=0)
     planes = padded_2(stacked, (("depth", 2),), 1)
@@ -91,15 +472,6 @@
         "rti,rc->tic", input_columns, pre_grad.reshape(-1, local_width), precision=highest
     )
     first_sum, second_sum = reduce_weight((first_raw, second_raw))
-    cells = (
-        inputs.shape[0]
-        * lax.axis_size("sample")
-        * inputs.shape[1]
-        * lax.axis_size("depth")
-        * inputs.shape[2]
-        * inputs.shape[3]
-    )
-    factor = 1.0 / math.sqrt(cells)
     return (input_grad, first_sum * factor, second_sum * factor)
 
 

time: 278 us -> 93.8 us (0.34)
  waiting for transfers between devices: 160 us -> 24.4 us
  local copies, waits for them, and re-layouts: 47.5 us -> 7.56 us
  Pallas kernels: 0 us -> 27.5 us
  matrix products: 24.7 us -> 0 us
  between operations: 14.6 us -> 0.89 us
  starting transfers between devices: 19.4 us -> 30.3 us
  other arithmetic: 8.71 us -> 2.68 us
    reduce_scatter x4 -> x0, waiting for transfers between devices: 113 us -> none  [the longest x2 95.1 us: reduce_weight(): return lax.psum_scatter(summed, 'depth', scatter_dimension=1, tiled=True)]
    psum x1 -> x0, waiting for transfers between devices: 41.5 us -> none  [reduce_weight(): summed = lax.psum(raw_pair, 'sample')]
    unnamed x116 -> x58, local copies, waits for them, and re-layouts: 40.8 us -> 7.56 us
    pallas_call x0 -> x6, Pallas kernels: none -> 27.5 us  [the longest x2 17 us: weight_call(): pl.pallas_call(functools.partial(weight_kernel, count, second, factor), g...]
    dot_general x4 -> x0, matrix products: 24.7 us -> none  [the longest x2 9.26 us: spread_back(): jnp.einsum('rtc,tic->ri', columns, kernel, precision=highest)]
    ppermute x6 -> x24, waiting for transfers between devices: 5.69 us -> 24.4 us  [the longest x9 12.2 us: around_depth(): lax.ppermute(field, 'depth', [(i, (i + step) % count) for i in range(coun...]
    ppermute x6 -> x24, starting transfers between devices: 19 us -> 30.3 us  [the longest x9 13.8 us: around_depth(): lax.ppermute(field, 'depth', [(i, (i + step) % count) for i in range(coun...]
    concatenate x5 -> x0, other arithmetic: 4.05 us -> none  [padded_2(): jnp.concatenate([lax.ppermute(tail, axis, [(i, (i + 1) % count) for i in...]
  transfers between devices with their start and end apart: 11 -> 24, of which waited for: 10 -> 11; matrix products, arithmetic and copies ran while one was open for 23% -> 3% of each run, Pallas kernels for 0% -> 14%
where the time goes in v1:
time: 93.8 us; the launch traced here: 93.4 us
  starting transfers between devices  30.3 us (32%)
  Pallas kernels  27.5 us (29%)
  waiting for transfers between devices  24.4 us (26%)
  local copies, waits for them, and re-layouts  7.56 us (8%)
  other arithmetic  2.68 us (3%)
    pallas_call x2, Pallas kernels, weight_call(): pl.pallas_call(functools.partial(weight_kernel, count, second, factor), g...  17 us
    ppermute x9, starting transfers between devices, around_depth(): lax.ppermute(field, 'depth', [(i, (i + step) % count) for i in range(coun...  13.8 us
    ppermute x9, waiting for transfers between devices, around_depth(): lax.ppermute(field, 'depth', [(i, (i + step) % count) for i in range(coun...  12.2 us
    ppermute x6, waiting for transfers between devices, across_samples(): lax.ppermute(field, 'sample', [(i, i ^ step) for i in range(count)])  10.3 us
    ppermute x3, starting transfers between devices, owners_across_samples(): moved.append(lax.ppermute(pair, ('depth', 'sample', 'filter'), links))  9.33 us
    unnamed x58, local copies, waits for them, and re-layouts  7.56 us
    pallas_call x2, Pallas kernels, spread_call(): pl.pallas_call(body, grid=(3,), in_specs=[full_spec(field.shape), pl.Bloc...  6.84 us
    ppermute x6, starting transfers between devices, across_samples(): lax.ppermute(field, 'sample', [(i, i ^ step) for i in range(count)])  6.45 us
  transfers between devices with their start and end apart: 24, of which 11 were waited for; matrix products, arithmetic and copies ran while one was open for 3% of the time, Pallas kernels for 14%

profile of v1, /device:TPU:0, one launch (start us, length us, event | category | flops | bytes accessed | tf_op | source)
XLA Modules:
  0.0 93.4 jit_solution(2665484717923667663)
XLA Ops:
  0.6 3.1 %collective-permute-start = (f32[2,8,8,128]{3,2,1,0:T(8,128)}, f32[2,8,8,128]{3,2,1,0:T(8,128)S(1)}, u32[]{:S(2)}, u32[]{:S(2)}) collective-permute-start(f32[2,8,8,128]{3,2,1,0:T(8,128)} %bitcast.7), channel_id=1, source_target_pairs={{0,8},{8,16},{16,24},{24,0},{1,9},{9,17},{17,25},{25,1},{2,10},{10... | collective-permute-start | bytes 196616 | tf_op jit(solution)/shard_map/ppermute | solution.py:394
  3.7 2.6 %collective-permute-start.1 = (f32[2,8,8,128]{3,2,1,0:T(8,128)}, f32[2,8,8,128]{3,2,1,0:T(8,128)S(1)}, u32[]{:S(2)}, u32[]{:S(2)}) collective-permute-start(f32[2,8,8,128]{3,2,1,0:T(8,128)} %bitcast.8), channel_id=1, source_target_pairs={{0,16},{8,24},{16,0},{24,8},{1,17},{9,25},{17,1},{25,9},{2,18},{10... | collective-permute-start | bytes 196616 | tf_op jit(solution)/shard_map/ppermute | solution.py:394
  6.3 1.3 %collective-permute-start.2 = (f32[2,8,8,128]{3,2,1,0:T(8,128)}, f32[2,8,8,128]{3,2,1,0:T(8,128)S(1)}, u32[]{:S(2)}, u32[]{:S(2)}) collective-permute-start(f32[2,8,8,128]{3,2,1,0:T(8,128)} %bitcast.9), channel_id=1, source_target_pairs={{0,24},{8,0},{16,8},{24,16},{1,25},{9,1},{17,9},{25,17},{2,26},{10... | collective-permute-start | bytes 196616 | tf_op jit(solution)/shard_map/ppermute | solution.py:394
  7.7 0.8 collective-permute-done.refs_1_
  8.4 2.6 %collective-permute-done.1.refs_2_ = f32[2,8,8,128]{3,2,1,0:T(8,128)S(1)} collective-permute-done((f32[2,8,8,128]{3,2,1,0:T(8,128)}, f32[2,8,8,128]{3,2,1,0:T(8,128)S(1)}, u32[]{:S(2)}, u32[]{:S(2)}) %collective-permute-start.1) | collective-permute-done | bytes 65568 | tf_op jit(solution)/shard_map/ppermute | solution.py:394
  11.0 0.2 collective-permute-done.2.refs_3_
  11.3 0.4 copy-done.14
  11.7 0.6 copy-done.15
  12.3 1.7 %join_depth.1.field_ref.refs_0_ = f32[8,8,8,128]{3,2,1,0:T(8,128)} custom-call(f32[2,8,8,128]{3,2,1,0:T(8,128)} %bitcast.10, f32[2,8,8,128]{3,2,1,0:T(8,128)} %copy-done.13, f32[2,8,8,128]{3,2,1,0:T(8,128)} %copy-done.14, f32[2,8,8,128]{3,2,1,0:T(8,128)} %copy-done.15), custom_call_target="tpu_custom_call" | custom-call | tf_op jit(solution)/shard_map/join_depth/pallas_call | solution.py:272
  13.9 0.9 %copy-done.3 = f32[8,8,8,128]{3,2,1,0:T(8,128)S(1)} copy-done((f32[8,8,8,128]{3,2,1,0:T(8,128)S(1)}, f32[8,8,8,128]{3,2,1,0:T(8,128)}, u32[]{:S(2)}) %copy-start.3) | copy-done | bytes 262168
  14.9 2.0 %copy-done.5 = f32[27,256,128]{2,1,0:T(8,128)S(1)} copy-done((f32[27,256,128]{2,1,0:T(8,128)S(1)}, f32[27,256,128]{2,1,0:T(8,128)}, u32[]{:S(2)}) %copy-start.5) | copy-done | bytes 3538968
  16.9 4.7 %act_back.1 = (f32[512,128]{1,0:T(8,128)S(1)}, f32[512,128]{1,0:T(8,128)}) custom-call(f32[8,8,8,128]{3,2,1,0:T(8,128)S(1)} %copy-done.3, f32[27,256,128]{2,1,0:T(8,128)S(1)} %copy-done.5), custom_call_target="tpu_custom_call" | custom-call | flops 2717908992 | bytes 3538944 | tf_op jit(solution)/shard_map/act_back/pallas_call | solution.py:241
  21.6 0.7 copy-done.2
  22.3 1.2 %collective-permute-start.4 = (f32[2,8,8,128]{3,2,1,0:T(8,128)S(1)}, f32[2,8,8,128]{3,2,1,0:T(8,128)S(1)}, u32[]{:S(2)}, u32[]{:S(2)}) collective-permute-start(f32[2,8,8,128]{3,2,1,0:T(8,128)S(1)} %bitcast.12), channel_id=1, source_target_pairs={{0,8},{8,16},{16,24},{24,0},{1,9},{9,17},{17,25},{25,1},{2,10},{10... | collective-permute-start | bytes 196616 | tf_op jit(solution)/shard_map/ppermute | solution.py:394
  23.5 2.6 %collective-permute-start.5 = (f32[2,8,8,128]{3,2,1,0:T(8,128)S(1)}, f32[2,8,8,128]{3,2,1,0:T(8,128)S(1)}, u32[]{:S(2)}, u32[]{:S(2)}) collective-permute-start(f32[2,8,8,128]{3,2,1,0:T(8,128)S(1)} %bitcast.13), channel_id=1, source_target_pairs={{0,16},{8,24},{16,0},{24,8},{1,17},{9,25},{17,1},{25,9},{2,18},{10... | collective-permute-start | bytes 196616 | tf_op jit(solution)/shard_map/ppermute | solution.py:394
  26.1 0.1 collective-permute-start.6
  26.2 1.9 %collective-permute-start.7 = (f32[2,8,8,128]{3,2,1,0:T(8,128)S(1)}, f32[2,8,8,128]{3,2,1,0:T(8,128)S(1)}, u32[]{:S(2)}, u32[]{:S(2)}) collective-permute-start(f32[2,8,8,128]{3,2,1,0:T(8,128)S(1)} %bitcast.16), channel_id=1, source_target_pairs={{0,8},{8,16},{16,24},{24,0},{1,9},{9,17},{17,25},{25,1},{2,10},{10... | collective-permute-start | bytes 196616 | tf_op jit(solution)/shard_map/ppermute | solution.py:394
  28.1 1.0 %collective-permute-done.4.refs_1_ = f32[2,8,8,128]{3,2,1,0:T(8,128)S(1)} collective-permute-done((f32[2,8,8,128]{3,2,1,0:T(8,128)S(1)}, f32[2,8,8,128]{3,2,1,0:T(8,128)S(1)}, u32[]{:S(2)}, u32[]{:S(2)}) %collective-permute-start.4) | collective-permute-done | bytes 65568 | tf_op jit(solution)/shard_map/ppermute | solution.py:394
  29.1 4.8 %collective-permute-done.5.refs_2_ = f32[2,8,8,128]{3,2,1,0:T(8,128)S(1)} collective-permute-done((f32[2,8,8,128]{3,2,1,0:T(8,128)S(1)}, f32[2,8,8,128]{3,2,1,0:T(8,128)S(1)}, u32[]{:S(2)}, u32[]{:S(2)}) %collective-permute-start.5) | collective-permute-done | bytes 65568 | tf_op jit(solution)/shard_map/ppermute | solution.py:394
  33.9 0.9 collective-permute-start.9
  34.8 2.3 %collective-permute-done.8.refs_6_ = f32[2,8,8,128]{3,2,1,0:T(8,128)S(1)} collective-permute-done((f32[2,8,8,128]{3,2,1,0:T(8,128)S(1)}, f32[2,8,8,128]{3,2,1,0:T(8,128)S(1)}, u32[]{:S(2)}, u32[]{:S(2)}) %collective-permute-start.8) | collective-permute-done | bytes 65568 | tf_op jit(solution)/shard_map/ppermute | solution.py:394
  37.1 0.6 copy-done.12
  37.8 0.5 collective-permute-done.9.refs_7_
  38.3 2.0 %activation.1 = (f32[8,8,8,128]{3,2,1,0:T(8,128)}, f32[8,8,8,128]{3,2,1,0:T(8,128)}) custom-call(f32[2,8,8,128]{3,2,1,0:T(8,128)} %bitcast.11, f32[2,8,8,128]{3,2,1,0:T(8,128)} %copy-done.8, f32[2,8,8,128]{3,2,1,0:T(8,128)} %copy-done.9, f32[2,8,8,128]{3,2,1,0:T(8,128)} %copy-done.10, f32[2,8,8,128]{3,2,1,0:T(8,128)} %bitcast.15, ...), custom_call_target="tpu_custom_call" | custom-call | tf_op jit(solution)/shard_map/activation/pallas_call | solution.py:303
  40.3 3.2 %collective-permute-start.14 = (f32[8,8,8,128]{3,2,1,0:T(8,128)}, f32[8,8,8,128]{3,2,1,0:T(8,128)S(1)}, u32[]{:S(2)}, u32[]{:S(2)}) collective-permute-start(f32[8,8,8,128]{3,2,1,0:T(8,128)} %get-tuple-element.14.refs_4_), channel_id=1, source_target_pairs={{0,2},{2,0},{4,6},{6,4},{8,10},{10,8},{12,14},{14,12},{17,19},{19,... | collective-permute-start | bytes 786440 | tf_op jit(solution)/shard_map/ppermute | solution.py:418
  43.5 3.4 %collective-permute-start.15 = (f32[8,8,8,128]{3,2,1,0:T(8,128)}, f32[8,8,8,128]{3,2,1,0:T(8,128)S(1)}, u32[]{:S(2)}, u32[]{:S(2)}) collective-permute-start(f32[8,8,8,128]{3,2,1,0:T(8,128)} %get-tuple-element.14.refs_4_), channel_id=1, source_target_pairs={{0,4},{2,6},{4,0},{6,2},{8,12},{10,14},{12,8},{14,10},{17,21},{19,... | collective-permute-start | bytes 786440 | tf_op jit(solution)/shard_map/ppermute | solution.py:418
  46.9 2.7 %collective-permute-start.16 = (f32[8,8,8,128]{3,2,1,0:T(8,128)}, f32[8,8,8,128]{3,2,1,0:T(8,128)S(1)}, u32[]{:S(2)}, u32[]{:S(2)}) collective-permute-start(f32[8,8,8,128]{3,2,1,0:T(8,128)} %get-tuple-element.14.refs_4_), channel_id=1, source_target_pairs={{0,6},{2,4},{4,2},{6,0},{8,14},{10,12},{12,10},{14,8},{17,23},{19,... | collective-permute-start | bytes 786440 | tf_op jit(solution)/shard_map/ppermute | solution.py:418
  49.7 1.2 %collective-permute-start.21 = (f32[8,8,8,128]{3,2,1,0:T(8,128)}, f32[8,8,8,128]{3,2,1,0:T(8,128)S(1)}, u32[]{:S(2)}, u32[]{:S(2)}) collective-permute-start(f32[8,8,8,128]{3,2,1,0:T(8,128)} %join_depth.1.field_ref.refs_0_), channel_id=1, source_target_pairs={{0,2},{2,0},{4,6},{6,4},{1,3},{3,1},{5,7},{7,5},{8,10},{10,8},{12,... | collective-permute-start | bytes 786440 | tf_op jit(solution)/shard_map/ppermute | solution.py:403
  50.9 1.1 %add.6 = f32[512,128]{1,0:T(8,128)S(1)} add(f32[512,128]{1,0:T(8,128)} %copy-done.2, f32[512,128]{1,0:T(8,128)} %collective-permute-done.3) | non-fusion elementwise | flops 65536 | bytes 786432 | tf_op jit(solution)/shard_map/add | solution.py:433
  52.0 1.0 %mul.3.field_ref.refs_0_ = f32[8,8,8,128]{3,2,1,0:T(8,128)S(1)} multiply(f32[8,8,8,128]{3,2,1,0:T(8,128)S(1)} %bitcast.5, f32[8,8,8,128]{3,2,1,0:T(8,128)} %get-tuple-element.11) | non-fusion elementwise | flops 65536 | bytes 786432 | tf_op jit(solution)/shard_map/mul | solution.py:433
  53.0 2.2 %input_back.1 = (f32[128,128]{1,0:T(8,128)S(1)}, f32[128,128]{1,0:T(8,128)S(1)}) custom-call(f32[8,8,8,128]{3,2,1,0:T(8,128)S(1)} %mul.3.field_ref.refs_0_, f32[27,256,128]{2,1,0:T(8,128)S(1)} %copy-done), custom_call_target="tpu_custom_call" | custom-call | flops 679477248 | bytes 3538944 | tf_op jit(solution)/shard_map/input_back/pallas_call | solution.py:241
  55.2 0.2 collective-permute-start.10
  55.4 1.6 %collective-permute-start.22 = (f32[8,8,8,128]{3,2,1,0:T(8,128)S(1)}, f32[8,8,8,128]{3,2,1,0:T(8,128)S(1)}, u32[]{:S(2)}, u32[]{:S(2)}) collective-permute-start(f32[8,8,8,128]{3,2,1,0:T(8,128)S(1)} %copy-done.4), channel_id=1, source_target_pairs={{0,4},{2,6},{4,0},{6,2},{1,5},{3,7},{5,1},{7,3},{8,12},{10,14},{12... | collective-permute-start | bytes 786440 | tf_op jit(solution)/shard_map/ppermute | solution.py:403
  57.0 1.9 %collective-permute-done.16.refs_7_ = f32[8,8,8,128]{3,2,1,0:T(8,128)S(1)} collective-permute-done((f32[8,8,8,128]{3,2,1,0:T(8,128)}, f32[8,8,8,128]{3,2,1,0:T(8,128)S(1)}, u32[]{:S(2)}, u32[]{:S(2)}) %collective-permute-start.16) | collective-permute-done | bytes 262176 | tf_op jit(solution)/shard_map/ppermute | solution.py:418
  58.9 0.1 collective-permute-start.23
  59.1 3.2 %collective-permute-done.21.refs_1_ = f32[8,8,8,128]{3,2,1,0:T(8,128)S(1)} collective-permute-done((f32[8,8,8,128]{3,2,1,0:T(8,128)}, f32[8,8,8,128]{3,2,1,0:T(8,128)S(1)}, u32[]{:S(2)}, u32[]{:S(2)}) %collective-permute-start.21) | collective-permute-done | bytes 262176 | tf_op jit(solution)/shard_map/ppermute | solution.py:403
  62.3 0.5 collective-permute-start.20
  62.8 0.6 add.7
  63.4 6.5 %collective-permute-done.22.refs_2_ = f32[8,8,8,128]{3,2,1,0:T(8,128)S(1)} collective-permute-done((f32[8,8,8,128]{3,2,1,0:T(8,128)S(1)}, f32[8,8,8,128]{3,2,1,0:T(8,128)S(1)}, u32[]{:S(2)}, u32[]{:S(2)}) %collective-permute-start.22) | collective-permute-done | bytes 262176 | tf_op jit(solution)/shard_map/ppermute | solution.py:403
  69.9 0.6 collective-permute-start.11
  70.5 1.2 %collective-permute-start.12 = (f32[8,8,8,128]{3,2,1,0:T(8,128)S(1)}, f32[8,8,8,128]{3,2,1,0:T(8,128)S(1)}, u32[]{:S(2)}, u32[]{:S(2)}) collective-permute-start(f32[8,8,8,128]{3,2,1,0:T(8,128)S(1)} %mul.3.field_ref.refs_0_), channel_id=1, source_target_pairs={{0,4},{2,6},{4,0},{6,2},{1,5},{3,7},{5,1},{7,3},{8,12},{10,14},{12... | collective-permute-start | bytes 786440 | tf_op jit(solution)/shard_map/ppermute | solution.py:403
  71.7 1.7 %collective-permute-start.13 = (f32[8,8,8,128]{3,2,1,0:T(8,128)S(1)}, f32[8,8,8,128]{3,2,1,0:T(8,128)S(1)}, u32[]{:S(2)}, u32[]{:S(2)}) collective-permute-start(f32[8,8,8,128]{3,2,1,0:T(8,128)S(1)} %mul.3.field_ref.refs_0_), channel_id=1, source_target_pairs={{0,6},{2,4},{4,2},{6,0},{1,7},{3,5},{5,3},{7,1},{8,14},{10,12},{12... | collective-permute-start | bytes 786440 | tf_op jit(solution)/shard_map/ppermute | solution.py:403
  73.5 0.6 copy-done.23
  74.1 0.7 copy-done.25
  74.8 8.5 %second_weight.1 = f32[27,64,128]{2,1,0:T(8,128)} custom-call(f32[8,8,8,128]{3,2,1,0:T(8,128)} %join_depth.1.field_ref.refs_0_, f32[8,8,8,128]{3,2,1,0:T(8,128)} %copy-done.20, f32[8,8,8,128]{3,2,1,0:T(8,128)} %copy-done.22, f32[8,8,8,128]{3,2,1,0:T(8,128)} %copy-done.24, f32[8,8,8,128]{3,2,1,0:T(8,128)} %get-tuple-element.14.refs_4_, ...), custom_call_target="tpu_custom_call" | custom-call | flops 3623878656 | bytes 4194304 | tf_op jit(solution)/shard_map/second_weight/pallas_call | solution.py:373
  83.4 0.6 collective-permute-done.13.refs_3_
  84.2 0.7 copy-done.28
  84.9 8.5 %first_weight.1 = f32[27,64,128]{2,1,0:T(8,128)} custom-call(f32[8,8,8,128]{3,2,1,0:T(8,128)} %copy-done.1, f32[8,8,8,128]{3,2,1,0:T(8,128)} %copy-done.26, f32[8,8,8,128]{3,2,1,0:T(8,128)} %copy-done.27, f32[8,8,8,128]{3,2,1,0:T(8,128)} %copy-done.28, f32[8,8,8,128]{3,2,1,0:T(8,128)} %get-tuple-element.14.refs_4_, f32[8,8,8,128]{3,2,1,0:T(8,128)} %copy-done.16, ...), custom_call_target="tpu_custom_call" | custom-call | flops 3623878656 | bytes 4194304 | tf_op jit(solution)/shard_map/first_weight/pallas_call | solution.py:373
  (67 shorter events, 0.4 us)
Async XLA Ops:
  0.6 7.8 %collective-permute-start = (f32[2,8,8,128]{3,2,1,0:T(8,128)}, f32[2,8,8,128]{3,2,1,0:T(8,128)S(1)}, u32[]{:S(2)}, u32[]{:S(2)}) collective-permute-start(f32[2,8,8,128]{3,2,1,0:T(8,128)} %bitcast.7), channel_id=1, source_target_pairs={{0,8},{8,16},{16,24},{24,0},{1,9},{9,17},{17,25},{25,1},{2,10},{10... | collective-permute-start | bytes 196616 | tf_op jit(solution)/shard_map/ppermute | solution.py:394
  3.7 7.3 %collective-permute-start.1 = (f32[2,8,8,128]{3,2,1,0:T(8,128)}, f32[2,8,8,128]{3,2,1,0:T(8,128)S(1)}, u32[]{:S(2)}, u32[]{:S(2)}) collective-permute-start(f32[2,8,8,128]{3,2,1,0:T(8,128)} %bitcast.8), channel_id=1, source_target_pairs={{0,16},{8,24},{16,0},{24,8},{1,17},{9,25},{17,1},{25,9},{2,18},{10... | collective-permute-start | bytes 196616 | tf_op jit(solution)/shard_map/ppermute | solution.py:394
  6.3 4.9 %collective-permute-start.2 = (f32[2,8,8,128]{3,2,1,0:T(8,128)}, f32[2,8,8,128]{3,2,1,0:T(8,128)S(1)}, u32[]{:S(2)}, u32[]{:S(2)}) collective-permute-start(f32[2,8,8,128]{3,2,1,0:T(8,128)} %bitcast.9), channel_id=1, source_target_pairs={{0,24},{8,0},{16,8},{24,16},{1,25},{9,1},{17,9},{25,17},{2,26},{10... | collective-permute-start | bytes 196616 | tf_op jit(solution)/shard_map/ppermute | solution.py:394
  8.4 2.8 %copy-start.13 = (f32[2,8,8,128]{3,2,1,0:T(8,128)}, f32[2,8,8,128]{3,2,1,0:T(8,128)S(1)}, u32[]{:S(2)}) copy-start(f32[2,8,8,128]{3,2,1,0:T(8,128)S(1)} %collective-permute-done.refs_1_) | copy-start | bytes 196612
  13.9 0.9 %copy-start.3 = (f32[8,8,8,128]{3,2,1,0:T(8,128)S(1)}, f32[8,8,8,128]{3,2,1,0:T(8,128)}, u32[]{:S(2)}) copy-start(f32[8,8,8,128]{3,2,1,0:T(8,128)} %join_depth.1.field_ref.refs_0_) | copy-start | bytes 786436
  14.9 2.0 %copy-start.5 = (f32[27,256,128]{2,1,0:T(8,128)S(1)}, f32[27,256,128]{2,1,0:T(8,128)}, u32[]{:S(2)}) copy-start(f32[27,256,128]{2,1,0:T(8,128)} %weight_ref.2) | copy-start | bytes 10616836
  16.9 5.4 %copy-start.6 = (f32[1,2,8,8,128]{4,3,2,1,0:T(8,128)S(1)}, f32[1,2,8,8,128]{4,3,2,1,0:T(8,128)}, u32[]{:S(2)}) copy-start(f32[1,2,8,8,128]{4,3,2,1,0:T(8,128)} %param.5) | copy-start | bytes 196612
  16.9 9.3 %copy-start.7 = (f32[1,2,8,8,128]{4,3,2,1,0:T(8,128)S(1)}, f32[1,2,8,8,128]{4,3,2,1,0:T(8,128)}, u32[]{:S(2)}) copy-start(f32[1,2,8,8,128]{4,3,2,1,0:T(8,128)} %param.6) | copy-start | bytes 196612
  16.9 36.1 %copy-start = (f32[27,256,128]{2,1,0:T(8,128)S(1)}, f32[27,256,128]{2,1,0:T(8,128)}, u32[]{:S(2)}) copy-start(f32[27,256,128]{2,1,0:T(8,128)} %weight_ref.3) | copy-start | bytes 10616836
  22.3 27.4 %collective-permute-start.3 = (f32[512,128]{1,0:T(8,128)}, f32[512,128]{1,0:T(8,128)}, u32[]{:S(2)}, u32[]{:S(2)}) collective-permute-start(f32[512,128]{1,0:T(8,128)} %get-tuple-element.10), channel_id=1, source_target_pairs={{0,1},{1,0},{2,3},{3,2},{4,5},{5,4},{6,7},{7,6},{8,9},{9,8},{10,11... | collective-permute-start | bytes 786440 | tf_op jit(solution)/shard_map/ppermute | solution.py:423
  22.3 6.9 %collective-permute-start.4 = (f32[2,8,8,128]{3,2,1,0:T(8,128)S(1)}, f32[2,8,8,128]{3,2,1,0:T(8,128)S(1)}, u32[]{:S(2)}, u32[]{:S(2)}) collective-permute-start(f32[2,8,8,128]{3,2,1,0:T(8,128)S(1)} %bitcast.12), channel_id=1, source_target_pairs={{0,8},{8,16},{16,24},{24,0},{1,9},{9,17},{17,25},{25,1},{2,10},{10... | collective-permute-start | bytes 196616 | tf_op jit(solution)/shard_map/ppermute | solution.py:394
  23.5 10.4 %collective-permute-start.5 = (f32[2,8,8,128]{3,2,1,0:T(8,128)S(1)}, f32[2,8,8,128]{3,2,1,0:T(8,128)S(1)}, u32[]{:S(2)}, u32[]{:S(2)}) collective-permute-start(f32[2,8,8,128]{3,2,1,0:T(8,128)S(1)} %bitcast.13), channel_id=1, source_target_pairs={{0,16},{8,24},{16,0},{24,8},{1,17},{9,25},{17,1},{25,9},{2,18},{10... | collective-permute-start | bytes 196616 | tf_op jit(solution)/shard_map/ppermute | solution.py:394
  26.1 8.7 %collective-permute-start.6 = (f32[2,8,8,128]{3,2,1,0:T(8,128)S(1)}, f32[2,8,8,128]{3,2,1,0:T(8,128)S(1)}, u32[]{:S(2)}, u32[]{:S(2)}) collective-permute-start(f32[2,8,8,128]{3,2,1,0:T(8,128)S(1)} %bitcast.14), channel_id=1, source_target_pairs={{0,24},{8,0},{16,8},{24,16},{1,25},{9,1},{17,9},{25,17},{2,26},{10... | collective-permute-start | bytes 196616 | tf_op jit(solution)/shard_map/ppermute | solution.py:394
  26.2 8.5 %collective-permute-start.7 = (f32[2,8,8,128]{3,2,1,0:T(8,128)S(1)}, f32[2,8,8,128]{3,2,1,0:T(8,128)S(1)}, u32[]{:S(2)}, u32[]{:S(2)}) collective-permute-start(f32[2,8,8,128]{3,2,1,0:T(8,128)S(1)} %bitcast.16), channel_id=1, source_target_pairs={{0,8},{8,16},{16,24},{24,0},{1,9},{9,17},{17,25},{25,1},{2,10},{10... | collective-permute-start | bytes 196616 | tf_op jit(solution)/shard_map/ppermute | solution.py:394
  29.1 8.0 %copy-start.8 = (f32[2,8,8,128]{3,2,1,0:T(8,128)}, f32[2,8,8,128]{3,2,1,0:T(8,128)S(1)}, u32[]{:S(2)}) copy-start(f32[2,8,8,128]{3,2,1,0:T(8,128)S(1)} %collective-permute-done.4.refs_1_) | copy-start | bytes 196612
  29.1 8.0 %collective-permute-start.8 = (f32[2,8,8,128]{3,2,1,0:T(8,128)S(1)}, f32[2,8,8,128]{3,2,1,0:T(8,128)S(1)}, u32[]{:S(2)}, u32[]{:S(2)}) collective-permute-start(f32[2,8,8,128]{3,2,1,0:T(8,128)S(1)} %bitcast.17), channel_id=1, source_target_pairs={{0,16},{8,24},{16,0},{24,8},{1,17},{9,25},{17,1},{25,9},{2,18},{10... | collective-permute-start | bytes 196616 | tf_op jit(solution)/shard_map/ppermute | solution.py:394
  33.9 3.2 %copy-start.9 = (f32[2,8,8,128]{3,2,1,0:T(8,128)}, f32[2,8,8,128]{3,2,1,0:T(8,128)S(1)}, u32[]{:S(2)}) copy-start(f32[2,8,8,128]{3,2,1,0:T(8,128)S(1)} %collective-permute-done.5.refs_2_) | copy-start | bytes 196612
  33.9 4.4 %collective-permute-start.9 = (f32[2,8,8,128]{3,2,1,0:T(8,128)S(1)}, f32[2,8,8,128]{3,2,1,0:T(8,128)}, u32[]{:S(2)}, u32[]{:S(2)}) collective-permute-start(f32[2,8,8,128]{3,2,1,0:T(8,128)S(1)} %bitcast.18), channel_id=1, source_target_pairs={{0,24},{8,0},{16,8},{24,16},{1,25},{9,1},{17,9},{25,17},{2,26},{10... | collective-permute-start | bytes 196616 | tf_op jit(solution)/shard_map/ppermute | solution.py:394
  34.8 2.4 %copy-start.10 = (f32[2,8,8,128]{3,2,1,0:T(8,128)}, f32[2,8,8,128]{3,2,1,0:T(8,128)S(1)}, u32[]{:S(2)}) copy-start(f32[2,8,8,128]{3,2,1,0:T(8,128)S(1)} %collective-permute-done.6.refs_3_) | copy-start | bytes 196612
  34.8 2.4 %copy-start.11 = (f32[2,8,8,128]{3,2,1,0:T(8,128)}, f32[2,8,8,128]{3,2,1,0:T(8,128)S(1)}, u32[]{:S(2)}) copy-start(f32[2,8,8,128]{3,2,1,0:T(8,128)S(1)} %collective-permute-done.7.refs_5_) | copy-start | bytes 196612
  40.3 15.2 %copy-start.4 = (f32[8,8,8,128]{3,2,1,0:T(8,128)S(1)}, f32[8,8,8,128]{3,2,1,0:T(8,128)}, u32[]{:S(2)}) copy-start(f32[8,8,8,128]{3,2,1,0:T(8,128)} %join_depth.1.field_ref.refs_0_) | copy-start | bytes 786436
  40.3 14.9 %collective-permute-start.14 = (f32[8,8,8,128]{3,2,1,0:T(8,128)}, f32[8,8,8,128]{3,2,1,0:T(8,128)S(1)}, u32[]{:S(2)}, u32[]{:S(2)}) collective-permute-start(f32[8,8,8,128]{3,2,1,0:T(8,128)} %get-tuple-element.14.refs_4_), channel_id=1, source_target_pairs={{0,2},{2,0},{4,6},{6,4},{8,10},{10,8},{12,14},{14,12},{17,19},{19,... | collective-permute-start | bytes 786440 | tf_op jit(solution)/shard_map/ppermute | solution.py:418
  43.5 12.0 %collective-permute-start.15 = (f32[8,8,8,128]{3,2,1,0:T(8,128)}, f32[8,8,8,128]{3,2,1,0:T(8,128)S(1)}, u32[]{:S(2)}, u32[]{:S(2)}) collective-permute-start(f32[8,8,8,128]{3,2,1,0:T(8,128)} %get-tuple-element.14.refs_4_), channel_id=1, source_target_pairs={{0,4},{2,6},{4,0},{6,2},{8,12},{10,14},{12,8},{14,10},{17,21},{19,... | collective-permute-start | bytes 786440 | tf_op jit(solution)/shard_map/ppermute | solution.py:418
  46.9 12.0 %collective-permute-start.16 = (f32[8,8,8,128]{3,2,1,0:T(8,128)}, f32[8,8,8,128]{3,2,1,0:T(8,128)S(1)}, u32[]{:S(2)}, u32[]{:S(2)}) collective-permute-start(f32[8,8,8,128]{3,2,1,0:T(8,128)} %get-tuple-element.14.refs_4_), channel_id=1, source_target_pairs={{0,6},{2,4},{4,2},{6,0},{8,14},{10,12},{12,10},{14,8},{17,23},{19,... | collective-permute-start | bytes 786440 | tf_op jit(solution)/shard_map/ppermute | solution.py:418
  49.6 9.5 %collective-permute-start.17 = (f32[8,8,8,128]{3,2,1,0:T(8,128)}, f32[8,8,8,128]{3,2,1,0:T(8,128)S(1)}, u32[]{:S(2)}, u32[]{:S(2)}) collective-permute-start(f32[8,8,8,128]{3,2,1,0:T(8,128)} %get-tuple-element.14.refs_4_), channel_id=1, source_target_pairs={{0,1},{1,0},{2,3},{3,2},{4,5},{5,4},{6,7},{7,6},{8,9},{9,8},{10,11... | collective-permute-start | bytes 786440 | tf_op jit(solution)/shard_map/ppermute | solution.py:423
  49.7 12.5 %collective-permute-start.21 = (f32[8,8,8,128]{3,2,1,0:T(8,128)}, f32[8,8,8,128]{3,2,1,0:T(8,128)S(1)}, u32[]{:S(2)}, u32[]{:S(2)}) collective-permute-start(f32[8,8,8,128]{3,2,1,0:T(8,128)} %join_depth.1.field_ref.refs_0_), channel_id=1, source_target_pairs={{0,2},{2,0},{4,6},{6,4},{1,3},{3,1},{5,7},{7,5},{8,10},{10,8},{12,... | collective-permute-start | bytes 786440 | tf_op jit(solution)/shard_map/ppermute | solution.py:403
  53.0 30.4 %copy-start.1 = (f32[8,8,8,128]{3,2,1,0:T(8,128)}, f32[8,8,8,128]{3,2,1,0:T(8,128)S(1)}, u32[]{:S(2)}) copy-start(f32[8,8,8,128]{3,2,1,0:T(8,128)S(1)} %mul.3.field_ref.refs_0_) | copy-start | bytes 786436
  55.2 18.2 %copy-start.16 = (f32[8,8,8,128]{3,2,1,0:T(8,128)}, f32[8,8,8,128]{3,2,1,0:T(8,128)S(1)}, u32[]{:S(2)}) copy-start(f32[8,8,8,128]{3,2,1,0:T(8,128)S(1)} %collective-permute-done.14.refs_5_) | copy-start | bytes 786436
  55.2 7.0 %collective-permute-start.10 = (f32[128,128]{1,0:T(8,128)S(1)}, f32[128,128]{1,0:T(8,128)S(1)}, u32[]{:S(2)}, u32[]{:S(2)}) collective-permute-start(f32[128,128]{1,0:T(8,128)S(1)} %get-tuple-element.13), channel_id=1, source_target_pairs={{0,1},{1,0},{2,3},{3,2},{4,5},{5,4},{6,7},{7,6},{8,9},{9,8},{10,11... | collective-permute-start | bytes 196616 | tf_op jit(solution)/shard_map/ppermute | solution.py:423
  55.4 18.0 %copy-start.17 = (f32[8,8,8,128]{3,2,1,0:T(8,128)}, f32[8,8,8,128]{3,2,1,0:T(8,128)S(1)}, u32[]{:S(2)}) copy-start(f32[8,8,8,128]{3,2,1,0:T(8,128)S(1)} %collective-permute-done.15.refs_6_) | copy-start | bytes 786436
  55.4 14.5 %collective-permute-start.22 = (f32[8,8,8,128]{3,2,1,0:T(8,128)S(1)}, f32[8,8,8,128]{3,2,1,0:T(8,128)S(1)}, u32[]{:S(2)}, u32[]{:S(2)}) collective-permute-start(f32[8,8,8,128]{3,2,1,0:T(8,128)S(1)} %copy-done.4), channel_id=1, source_target_pairs={{0,4},{2,6},{4,0},{6,2},{1,5},{3,7},{5,1},{7,3},{8,12},{10,14},{12... | collective-permute-start | bytes 786440 | tf_op jit(solution)/shard_map/ppermute | solution.py:403
  58.9 14.5 %copy-start.18 = (f32[8,8,8,128]{3,2,1,0:T(8,128)}, f32[8,8,8,128]{3,2,1,0:T(8,128)S(1)}, u32[]{:S(2)}) copy-start(f32[8,8,8,128]{3,2,1,0:T(8,128)S(1)} %collective-permute-done.16.refs_7_) | copy-start | bytes 786436
  58.9 11.6 %collective-permute-start.23 = (f32[8,8,8,128]{3,2,1,0:T(8,128)S(1)}, f32[8,8,8,128]{3,2,1,0:T(8,128)S(1)}, u32[]{:S(2)}, u32[]{:S(2)}) collective-permute-start(f32[8,8,8,128]{3,2,1,0:T(8,128)S(1)} %copy-done.4), channel_id=1, source_target_pairs={{0,6},{2,4},{4,2},{6,0},{1,7},{3,5},{5,3},{7,1},{8,14},{10,12},{12... | collective-permute-start | bytes 786440 | tf_op jit(solution)/shard_map/ppermute | solution.py:403
  59.1 14.4 %copy-start.19 = (f32[8,8,8,128]{3,2,1,0:T(8,128)}, f32[8,8,8,128]{3,2,1,0:T(8,128)S(1)}, u32[]{:S(2)}) copy-start(f32[8,8,8,128]{3,2,1,0:T(8,128)S(1)} %collective-permute-done.17.refs_8_) | copy-start | bytes 786436
  59.1 12.7 %collective-permute-start.18 = (f32[8,8,8,128]{3,2,1,0:T(8,128)S(1)}, f32[8,8,8,128]{3,2,1,0:T(8,128)S(1)}, u32[]{:S(2)}, u32[]{:S(2)}) collective-permute-start(f32[8,8,8,128]{3,2,1,0:T(8,128)S(1)} %collective-permute-done.14.refs_5_), channel_id=1, source_target_pairs={{0,1},{1,0},{2,3},{3,2},{4,5},{5,4},{6,7},{7,6},{8,9},{9,8},{10,11... | collective-permute-start | bytes 786440 | tf_op jit(solution)/shard_map/ppermute | solution.py:423
  62.2 11.2 %copy-start.20 = (f32[8,8,8,128]{3,2,1,0:T(8,128)}, f32[8,8,8,128]{3,2,1,0:T(8,128)S(1)}, u32[]{:S(2)}) copy-start(f32[8,8,8,128]{3,2,1,0:T(8,128)S(1)} %collective-permute-done.21.refs_1_) | copy-start | bytes 786436
  62.2 11.2 %collective-permute-start.19 = (f32[8,8,8,128]{3,2,1,0:T(8,128)S(1)}, f32[8,8,8,128]{3,2,1,0:T(8,128)S(1)}, u32[]{:S(2)}, u32[]{:S(2)}) collective-permute-start(f32[8,8,8,128]{3,2,1,0:T(8,128)S(1)} %collective-permute-done.15.refs_6_), channel_id=1, source_target_pairs={{0,1},{1,0},{2,3},{3,2},{4,5},{5,4},{6,7},{7,6},{8,9},{9,8},{10,11... | collective-permute-start | bytes 786440 | tf_op jit(solution)/shard_map/ppermute | solution.py:423
  62.3 11.2 %collective-permute-start.20 = (f32[8,8,8,128]{3,2,1,0:T(8,128)S(1)}, f32[8,8,8,128]{3,2,1,0:T(8,128)S(1)}, u32[]{:S(2)}, u32[]{:S(2)}) collective-permute-start(f32[8,8,8,128]{3,2,1,0:T(8,128)S(1)} %collective-permute-done.16.refs_7_), channel_id=1, source_target_pairs={{0,1},{1,0},{2,3},{3,2},{4,5},{5,4},{6,7},{7,6},{8,9},{9,8},{10,11... | collective-permute-start | bytes 786440 | tf_op jit(solution)/shard_map/ppermute | solution.py:423
  69.9 3.6 %copy-start.22 = (f32[8,8,8,128]{3,2,1,0:T(8,128)}, f32[8,8,8,128]{3,2,1,0:T(8,128)S(1)}, u32[]{:S(2)}) copy-start(f32[8,8,8,128]{3,2,1,0:T(8,128)S(1)} %collective-permute-done.22.refs_2_) | copy-start | bytes 786436
  69.9 13.4 %collective-permute-start.11 = (f32[8,8,8,128]{3,2,1,0:T(8,128)S(1)}, f32[8,8,8,128]{3,2,1,0:T(8,128)S(1)}, u32[]{:S(2)}, u32[]{:S(2)}) collective-permute-start(f32[8,8,8,128]{3,2,1,0:T(8,128)S(1)} %mul.3.field_ref.refs_0_), channel_id=1, source_target_pairs={{0,2},{2,0},{4,6},{6,4},{1,3},{3,1},{5,7},{7,5},{8,10},{10,8},{12,... | collective-permute-start | bytes 786440 | tf_op jit(solution)/shard_map/ppermute | solution.py:403
  70.5 3.0 %copy-start.24 = (f32[8,8,8,128]{3,2,1,0:T(8,128)}, f32[8,8,8,128]{3,2,1,0:T(8,128)S(1)}, u32[]{:S(2)}) copy-start(f32[8,8,8,128]{3,2,1,0:T(8,128)S(1)} %collective-permute-done.23.refs_3_) | copy-start | bytes 786436
  70.5 12.8 %collective-permute-start.12 = (f32[8,8,8,128]{3,2,1,0:T(8,128)S(1)}, f32[8,8,8,128]{3,2,1,0:T(8,128)S(1)}, u32[]{:S(2)}, u32[]{:S(2)}) collective-permute-start(f32[8,8,8,128]{3,2,1,0:T(8,128)S(1)} %mul.3.field_ref.refs_0_), channel_id=1, source_target_pairs={{0,4},{2,6},{4,0},{6,2},{1,5},{3,7},{5,1},{7,3},{8,12},{10,14},{12... | collective-permute-start | bytes 786440 | tf_op jit(solution)/shard_map/ppermute | solution.py:403
  71.7 1.8 %copy-start.21 = (f32[8,8,8,128]{3,2,1,0:T(8,128)}, f32[8,8,8,128]{3,2,1,0:T(8,128)S(1)}, u32[]{:S(2)}) copy-start(f32[8,8,8,128]{3,2,1,0:T(8,128)S(1)} %collective-permute-done.18.refs_9_) | copy-start | bytes 786436
  71.7 12.2 %collective-permute-start.13 = (f32[8,8,8,128]{3,2,1,0:T(8,128)S(1)}, f32[8,8,8,128]{3,2,1,0:T(8,128)S(1)}, u32[]{:S(2)}, u32[]{:S(2)}) collective-permute-start(f32[8,8,8,128]{3,2,1,0:T(8,128)S(1)} %mul.3.field_ref.refs_0_), channel_id=1, source_target_pairs={{0,6},{2,4},{4,2},{6,0},{1,7},{3,5},{5,3},{7,1},{8,14},{10,12},{12... | collective-permute-start | bytes 786440 | tf_op jit(solution)/shard_map/ppermute | solution.py:403
  73.4 0.7 copy-start.23
  74.1 0.7 copy-start.25
  83.4 0.7 copy-start.26
  83.4 0.8 copy-start.27
  (5 other events, 3.3 us)

commit v2 on v1

--- a/solution.py
+++ b/solution.py
@@ -1,4 +1,5 @@
 import functools
+import itertools
 import math
 
 import jax
@@ -7,6 +8,7 @@
 from jax.experimental import pallas as pl
 from jax.experimental.pallas import tpu as pltpu
 from jax.sharding import PartitionSpec as P
+
 
 highest = lax.Precision.HIGHEST
 
@@ -79,7 +81,7 @@
     return lax.axis_size("depth"), lax.axis_size("sample"), lax.axis_size("filter")
 
 
-def gather_plan_fits(inputs, output_grad, second_weight):
+def gather_plan_fits(output_grad, second_weight):
     depths, samples, halves = axis_sizes()
     batch, planes, height, breadth, lanes = output_grad.shape
     rows = batch * samples * planes * depths * height * breadth
@@ -140,26 +142,24 @@
     return value.reshape(-1, value.shape[-1])
 
 
-def back_step(first, planes, weight_ref, even_ref, odd_ref, cells_first):
-    height = weight_ref.shape[1]
+def back_step(first, planes, weight_ref, even_ref, odd_ref):
     total = None
     for row_tap in range(3):
-        left = []
-        right = []
+        cells = []
+        kernels = []
         for column_tap in range(3):
             kernel_high, kernel_low = two_parts(weight_ref[3 * row_tap + column_tap])
             cell = [
                 slab(even_ref, odd_ref, (2 - column_tap, part), first, planes, 2 - row_tap)
                 for part in range(2)
             ]
-            left += [cell[0], cell[1], cell[0]]
-            right += [kernel_high, kernel_high, kernel_low]
-        left = jnp.concatenate(left, axis=1)
-        right = jnp.concatenate(right, axis=1)
-        if not cells_first:
-            left, right = right, left
+            cells += [cell[0], cell[1], cell[0]]
+            kernels += [kernel_high, kernel_high, kernel_low]
         product = lax.dot_general(
-            left, right, (((1,), (1,)), ((), ())), preferred_element_type=jnp.float32
+            jnp.concatenate(kernels, axis=1),
+            jnp.concatenate(cells, axis=1),
+            (((1,), (1,)), ((), ())),
+            preferred_element_type=jnp.float32,
         )
         total = product if total is None else total + product
     return total
@@ -169,57 +169,45 @@
     width = keep_ref.shape[-1]
     mine = lax.axis_index("filter") == 0
     low, high = total[:, :width], total[:, width:]
-    keep_ref[...] = jnp.where(mine, low, high)
-    send_ref[...] = jnp.where(mine, high, low)
-
-
-def act_back_kernel(field_ref, weight_ref, keep_ref, send_ref, even_ref, odd_ref, total_ref):
-    step = pl.program_id(0)
-    planes = field_ref.shape[0]
-
-    @pl.when(step == 0)
-    def _():
-        for ref in (even_ref, odd_ref):
-            for tap in range(3):
-                for part in range(2):
-                    for plane in (0, planes + 1):
-                        ref[tap, part, plane] = jnp.zeros(ref.shape[3:], ref.dtype)
-        spread_field(
-            lambda plane: field_ref[plane],
-            planes,
-            even_ref.at[:, :, 1 : planes + 1],
-            odd_ref.at[:, :, 1 : planes + 1],
+    keep_ref[...] = jnp.where(mine, low, high).reshape(keep_ref.shape)
+    send_ref[...] = jnp.where(mine, high, low).reshape(send_ref.shape)
+
+
+def back_kernel(before_ref, own_ref, after_ref, weight_ref, keep_ref, send_ref, *scratch):
+    even_ref, odd_ref, total_ref, *fetched = scratch
+    planes = own_ref.shape[0]
+    group = weight_ref.shape[0] // 3
+    kernel_ref, semaphores = fetched or (weight_ref, None)
+
+    def fetch(step):
+        where = pl.ds(step * group, group)
+        return pltpu.make_async_copy(
+            weight_ref.at[where], kernel_ref.at[where], semaphores.at[step]
         )
-        total_ref[...] = jnp.zeros_like(total_ref)
-
-    total_ref[...] += back_step(2 - step, planes, weight_ref, even_ref, odd_ref, True)
-
-    @pl.when(step == 2)
-    def _():
-        split_halves(total_ref[...], keep_ref, send_ref)
-
-
-def input_back_kernel(planes, field_ref, weight_ref, keep_ref, send_ref, even_ref, odd_ref, total_ref):
-    step = pl.program_id(0)
-    depths = field_ref.shape[0]
-
-    @pl.when(step == 0)
-    def _():
-        first = lax.axis_index("depth") * planes
-
-        def plane_at(offset):
-            place = first + offset - 1
-            inside = (place >= 0) & (place < depths)
-            return jnp.where(inside, field_ref[jnp.clip(place, 0, depths - 1)], 0.0)
-
-        spread_field(plane_at, planes + 2, even_ref, odd_ref)
-        total_ref[...] = jnp.zeros_like(total_ref)
-
-    total_ref[...] += back_step(2 - step, planes, weight_ref, even_ref, odd_ref, False)
-
-    @pl.when(step == 2)
-    def _():
-        split_halves(total_ref[...].T, keep_ref, send_ref)
+
+    if fetched:
+        for step in range(3):
+            fetch(step).start()
+    place = lax.axis_index("depth")
+
+    def plane_at(offset):
+        if offset == 0:
+            return jnp.where(place > 0, before_ref[planes - 1], 0.0)
+        if offset == planes + 1:
+            return jnp.where(place < lax.axis_size("depth") - 1, after_ref[0], 0.0)
+        return own_ref[offset - 1]
+
+    spread_field(plane_at, planes + 2, even_ref, odd_ref)
+    total_ref[...] = jnp.zeros_like(total_ref)
+
+    @pl.loop(0, 3)
+    def _(step):
+        if fetched:
+            fetch(step).wait()
+        kernels = kernel_ref.at[pl.ds(step * group, group)]
+        total_ref[...] += back_step(2 - step, planes, kernels, even_ref, odd_ref)
+
+    split_halves(total_ref[...].T, keep_ref, send_ref)
 
 
 def full_spec(shape):
@@ -233,28 +221,51 @@
     ]
 
 
-def spread_call(field, kernel, planes, whole):
-    depths, height, breadth, lanes = field.shape
+def back_call(before, own, after, kernel, fetch):
+    planes, height, breadth, lanes = own.shape
     taps, ins, outs = kernel.shape
     rows = planes * height * breadth
-    body = act_back_kernel if whole else functools.partial(input_back_kernel, planes)
+    shape = own.shape[:3] + (ins // 2,)
     return pl.pallas_call(
-        body,
-        grid=(3,),
-        in_specs=[
-            full_spec(field.shape),
-            pl.BlockSpec((taps // 3, ins, outs), lambda step: (step, 0, 0)),
-        ],
-        out_specs=[full_spec((rows, ins // 2))] * 2,
-        out_shape=[jax.ShapeDtypeStruct((rows, ins // 2), jnp.float32)] * 2,
+        back_kernel,
+        in_specs=[pl.BlockSpec(memory_space=pltpu.VMEM)] * 3
+        + [pl.BlockSpec(memory_space=pltpu.HBM if fetch else pltpu.VMEM)],
+        out_shape=[jax.ShapeDtypeStruct(shape, jnp.float32)] * 2,
         scratch_shapes=spread_scratch(planes + 2, height, breadth, lanes, 2)
-        + [pltpu.VMEM((rows, ins) if whole else (ins, rows), jnp.float32)],
-        compiler_params=pltpu.CompilerParams(vmem_limit_bytes=48 * 2**20),
+        + [pltpu.VMEM((ins, rows), jnp.float32)]
+        + [pltpu.VMEM(kernel.shape, jnp.float32), pltpu.SemaphoreType.DMA((3,))] * fetch,
+        compiler_params=pltpu.CompilerParams(vmem_limit_bytes=(14 if fetch else 10) * 2**20),
         cost_estimate=pl.CostEstimate(
             flops=6 * rows * taps * ins * outs, transcendentals=0, bytes_accessed=4 * kernel.size
         ),
-        name="act_back" if whole else "input_back",
-    )(field, kernel)
+    )(before, own, after, pltpu.with_memory_space_constraint(kernel, pltpu.HBM) if fetch else kernel)
+
+
+def stage_kernel(inputs_ref, before_ref, grad_ref, both_ref, own_ref, semaphores):
+    copies = [
+        pltpu.make_async_copy(inputs_ref, both_ref.at[0], semaphores.at[0]),
+        pltpu.make_async_copy(before_ref, both_ref.at[1], semaphores.at[1]),
+        pltpu.make_async_copy(grad_ref, own_ref, semaphores.at[2]),
+    ]
+    for copy in copies:
+        copy.start()
+    for copy in copies:
+        copy.wait()
+
+
+def stage_call(inputs, before, grad):
+    return pl.pallas_call(
+        stage_kernel,
+        in_specs=[pl.BlockSpec(memory_space=pltpu.HBM)] * 3,
+        out_specs=[pl.BlockSpec(memory_space=pltpu.VMEM)] * 2,
+        out_shape=[
+            jax.ShapeDtypeStruct((2, *inputs.shape), jnp.float32),
+            jax.ShapeDtypeStruct(grad.shape, jnp.float32),
+        ],
+        scratch_shapes=[pltpu.SemaphoreType.DMA((3,))],
+        compiler_params=pltpu.CompilerParams(vmem_limit_bytes=2 * 2**20),
+        name="stage",
+    )(*(pltpu.with_memory_space_constraint(each, pltpu.HBM) for each in (inputs, before, grad)))
 
 
 def join_kernel(*refs):
@@ -272,59 +283,63 @@
     return pl.pallas_call(
         join_kernel,
         out_shape=jax.ShapeDtypeStruct((planes * len(pieces), *rest), jnp.float32),
+        compiler_params=pltpu.CompilerParams(vmem_limit_bytes=2 * 2**20),
         name="join_depth",
     )(*pieces)
 
 
-def activation_kernel(count, *refs):
-    saved, before = refs[:count], refs[count : 2 * count]
-    slope_ref, pair_ref = refs[2 * count :]
-    planes = saved[0].shape[0]
+def pair_kernel(count, *refs):
+    fields, outs = refs[:count], refs[count:]
+    depths = len(outs)
     place = lax.axis_index("depth")
-    lower = lax.rem(place, 2) == 0
-    half = saved[0].shape[-1] // 2
-    for step in range(count):
-        source = lax.rem(place + count - step, count)
-        where = pl.ds(source * planes, planes)
-        shape = saved[step].shape
-        first = saved[step][...].reshape(-1, shape[-1])
-        activated, slope = gelu_pair(before[step][...].reshape(-1, shape[-1]))
-        slope_ref[where] = slope.reshape(shape)
+    lanes = fields[0].shape[-1]
+    half = lanes // 2
+    for sample in range(count):
+        shape = fields[sample].shape[1:]
+        first = fields[sample][0].reshape(-1, lanes)
+        activated, _ = gelu_pair(fields[sample][1].reshape(-1, lanes))
         lane = lax.broadcasted_iota(jnp.int32, first.shape, 1)
-        low = jnp.where(lane < half, first, pltpu.roll(activated, half, axis=1))
-        high = jnp.where(lane < half, pltpu.roll(first, half, axis=1), activated)
-        pair_ref[where] = jnp.where(lower, low, high).reshape(shape)
-
-
-def activation_call(saved, before):
-    planes, *rest = saved[0].shape
-    count = len(saved)
-    shape = (planes * count, *rest)
+        low = jnp.where(lane < half, first, pltpu.roll(activated, half, axis=1)).reshape(shape)
+        high = jnp.where(lane < half, pltpu.roll(first, half, axis=1), activated).reshape(shape)
+        for step in range(depths):
+            lower = lax.rem(place + step, 2) == 0
+            outs[step][sample] = jnp.where(lower, low, high)
+
+
+def pair_call(fields):
+    depths, count = lax.axis_size("depth"), len(fields)
+    shape = (count, *fields[0].shape[1:])
     return pl.pallas_call(
-        functools.partial(activation_kernel, count),
-        out_shape=[jax.ShapeDtypeStruct(shape, jnp.float32)] * 2,
-        name="activation",
-    )(*saved, *before)
+        functools.partial(pair_kernel, count),
+        out_shape=[jax.ShapeDtypeStruct(shape, jnp.float32)] * depths,
+        compiler_params=pltpu.CompilerParams(vmem_limit_bytes=6 * 2**20),
+        name="pair",
+    )(*fields)
 
 
 def weight_kernel(count, second, factor, *refs):
-    fields, near, far = refs[:count], refs[count : 2 * count], refs[2 * count : 3 * count]
-    out_ref, even_ref, odd_ref, grad_ref = refs[3 * count :]
+    out_ref, even_ref, odd_ref, grad_ref = refs[-4:]
+    fields, pairs = refs[:count], refs[count:-4]
+    depths = len(pairs) // 2
+    near, far = pairs[:depths], pairs[depths:]
     step = pl.program_id(0)
-    planes, height, breadth, lanes = near[0].shape
+    planes, height, breadth, lanes = fields[0].shape
+    share = planes // depths
     half = lanes // 2
     rows = planes * height * breadth
 
     @pl.when(step == 0)
     def _():
-        owner = lax.axis_index("depth") // 2 == lax.axis_index("filter")
+        place = lax.axis_index("depth")
+        owner = place // 2 == lax.axis_index("filter")
         for sample in range(count):
             for ref in (even_ref, odd_ref):
                 for tap in range(3):
                     for plane in (0, planes + 1):
                         ref[tap, sample, plane] = jnp.zeros(ref.shape[3:], ref.dtype)
-            for plane in range(planes):
-                cells = jnp.where(owner, near[sample][plane], far[sample][plane])
+            for hop, index in itertools.product(range(depths), range(share)):
+                plane = lax.rem(place + depths - hop, depths) * share + index
+                cells = jnp.where(owner, near[hop][sample, index], far[hop][sample, index])
                 lane = lax.broadcasted_iota(jnp.int32, cells.shape, 2)
                 swapped = pltpu.roll(cells, half, axis=2)
                 lower = lane < half
@@ -362,7 +377,7 @@
 
 
 def weight_call(fields, near, far, second, factor):
-    planes, height, breadth, lanes = near[0].shape
+    planes, height, breadth, lanes = fields[0].shape
     count = len(fields)
     rows = planes * height * breadth
     scratch = [
@@ -373,11 +388,11 @@
     return pl.pallas_call(
         functools.partial(weight_kernel, count, second, factor),
         grid=(3,),
-        in_specs=[full_spec(near[0].shape)] * (3 * count),
+        in_specs=[full_spec(each.shape) for each in (*fields, *near, *far)],
         out_specs=pl.BlockSpec((9, lanes // 2, lanes), lambda step: (step, 0, 0)),
         out_shape=jax.ShapeDtypeStruct((27, lanes // 2, lanes), jnp.float32),
         scratch_shapes=scratch,
-        compiler_params=pltpu.CompilerParams(vmem_limit_bytes=56 * 2**20),
+        compiler_params=pltpu.CompilerParams(vmem_limit_bytes=20 * 2**20),
         cost_estimate=pl.CostEstimate(
             flops=4 * 2 * 27 * count * rows * lanes * lanes // 2,
             transcendentals=0,
@@ -389,33 +404,32 @@
 
 def around_depth(field):
     count = lax.axis_size("depth")
-    steps = [1, count - 1] + list(range(2, count - 1))
-    moved = {
-        step: lax.ppermute(field, "depth", [(i, (i + step) % count) for i in range(count)])
-        for step in steps
-    }
+    moved = {}
+    for step in [1, count - 1] + list(range(2, count - 1)):
+        links = [(i, (i + step) % count) for i in range(count)]
+        moved[step] = lax.ppermute(field, "depth", links)
     return [field] + [moved[step] for step in range(1, count)]
 
 
 def across_samples(field):
     count = lax.axis_size("sample")
-    return [field] + [
-        lax.ppermute(field, "sample", [(i, i ^ step) for i in range(count)])
-        for step in range(1, count)
-    ]
-
-
-def owners_across_samples(pair):
+    moved = [field]
+    for step in range(1, count):
+        moved.append(lax.ppermute(field, "sample", [(i, i ^ step) for i in range(count)]))
+    return moved
+
+
+def owners_around_depth(pairs):
     depths, samples, halves = axis_sizes()
-    moved = [pair]
-    for step in range(1, samples):
+    moved = [pairs[0]]
+    for step in range(1, depths):
         links = []
-        for depth in range(depths):
-            for sample in range(samples):
-                half = depth // 2
-                place = lambda value: (depth * samples + value) * halves + half
-                links.append((place(sample), place(sample ^ step)))
-        moved.append(lax.ppermute(pair, ("depth", "sample", "filter"), links))
+        for depth, sample in itertools.product(range(depths), range(samples)):
+            target = (depth + step) % depths
+            half = target // 2
+            place = lambda value: (value * samples + sample) * halves + half
+            links.append((place(depth), place(target)))
+        moved.append(lax.ppermute(pairs[step], ("depth", "sample", "filter"), links))
     return moved
 
 
@@ -425,17 +439,21 @@
 
 def gather_plan(inputs, pre_gelu, output_grad, first_weight, second_weight, factor):
     local_shape = output_grad.shape
-    planes = local_shape[1]
     inputs, pre_gelu, output_grad = inputs[0], pre_gelu[0], output_grad[0]
-    grads = join_depth(around_depth(output_grad))
-    slope, pair = activation_call(around_depth(inputs), around_depth(pre_gelu))
-    keep, send = spread_call(grads, second_weight, grads.shape[0], True)
-    pre_grad = (keep + swap_filter(send)).reshape(slope.shape) * slope
+    grads = around_depth(output_grad)
+    both, grads[0] = stage_call(inputs, pre_gelu, output_grad)
+    fields = across_samples(both)
+    keep, send = back_call(grads[1], grads[0], grads[-1], second_weight, True)
+    got = swap_filter(send)
+    pre_grad = (keep + got) * gelu_pair(both[1])[1]
+    grads = join_depth(grads)
     all_grads = across_samples(grads)
-    near = owners_across_samples(pair)
+    pre_grads = around_depth(pre_grad)
+    pairs = pair_call(fields)
+    near = owners_around_depth(pairs)
     far = [swap_filter(piece) for piece in near]
-    all_pre = across_samples(pre_grad)
-    keep, send = spread_call(pre_grad, first_weight, planes, False)
+    all_pre = across_samples(join_depth(pre_grads))
+    keep, send = back_call(pre_grads[1], pre_grads[0], pre_grads[-1], first_weight, False)
     input_grad = (keep + swap_filter(send)).reshape(local_shape)
     second = weight_call(all_grads, near, far, True, factor)
     first = weight_call(all_pre, near, far, False, factor)
@@ -452,8 +470,10 @@
         * inputs.shape[3]
     )
     factor = 1.0 / math.sqrt(cells)
-    if gather_plan_fits(inputs, output_grad, second_weight):
-        return gather_plan(inputs, pre_gelu, output_grad, first_weight, second_weight, factor)
+    if gather_plan_fits(output_grad, second_weight):
+        return gather_plan(
+            inputs, pre_gelu, output_grad, first_weight, second_weight, factor
+        )
     activated, slope = gelu_pair(pre_gelu)
     stacked = jnp.stack([inputs, activated], axis=0)
     planes = padded_2(stacked, (("depth", 2),), 1)

time: 93.8 us -> 66.9 us (0.71)
  waiting for transfers between devices: 24.4 us -> 12.5 us
  local copies, waits for them, and re-layouts: 7.56 us -> 0.01 us
  Pallas kernels: 27.5 us -> 20 us
  starting transfers between devices: 30.3 us -> 32.7 us
  other arithmetic: 2.68 us -> 0.68 us
    unnamed x58 -> x4, local copies, waits for them, and re-layouts: 7.56 us -> 0.01 us
    ppermute x12 -> x9, waiting for transfers between devices: 14.1 us -> 7.61 us  [the longest x3 5.37 us: owners_around_depth(): lax.ppermute(pairs[step], ('depth', 'sample', 'filter'), links)]
    ppermute x6 -> x9, starting transfers between devices: 6.45 us -> 12.8 us  [across_samples(): lax.ppermute(field, 'sample', [(i, i ^ step) for i in range(count)])]
    ppermute x12 -> x9, starting transfers between devices: 23.1 us -> 17.5 us  [the longest x6 11.9 us: around_depth(): moved[step] = lax.ppermute(field, 'depth', links)]
    ppermute x6 -> x9, waiting for transfers between devices: 10.3 us -> 4.91 us  [across_samples(): lax.ppermute(field, 'sample', [(i, i ^ step) for i in range(count)])]
    pallas_call x2, Pallas kernels: 17 us -> 13.3 us  [weight_call(): pl.pallas_call(functools.partial(weight_kernel, count, second, factor), g...]
    pallas_call x3 -> x4, Pallas kernels: 8.82 us -> 6.6 us  [the longest x2 5.45 us: back_call(): pl.pallas_call(back_kernel, in_specs=[pl.BlockSpec(memory_space=pltpu.VME...]
    add x2 -> x0, other arithmetic: 1.69 us -> none  [the longest x1 1.06 us: gather_plan(): pre_grad = (keep + swap_filter(send)).reshape(slope.shape) * slope]
  transfers between devices with their start and end apart: 24 -> 24, of which waited for: 11 -> 6; matrix products, arithmetic and copies ran while one was open for 3% -> 1% of each run, Pallas kernels for 14% -> 15%
where the time goes in v2:
time: 66.9 us; the launch traced here: 66.7 us
  starting transfers between devices  32.7 us (49%)
  Pallas kernels  20 us (30%)
  waiting for transfers between devices  12.5 us (19%)
  between operations  0.8 us (1%)
  other arithmetic  0.68 us (1%)
    pallas_call x2, Pallas kernels, weight_call(): pl.pallas_call(functools.partial(weight_kernel, count, second, factor), g...  13.3 us
    ppermute x9, starting transfers between devices, across_samples(): lax.ppermute(field, 'sample', [(i, i ^ step) for i in range(count)])  12.8 us
    ppermute x6, starting transfers between devices, around_depth(): moved[step] = lax.ppermute(field, 'depth', links)  11.9 us
    ppermute x3, starting transfers between devices, owners_around_depth(): lax.ppermute(pairs[step], ('depth', 'sample', 'filter'), links)  5.55 us
    pallas_call x2, Pallas kernels, back_call(): pl.pallas_call(back_kernel, in_specs=[pl.BlockSpec(memory_space=pltpu.VME...  5.45 us
    ppermute x3, waiting for transfers between devices, owners_around_depth(): lax.ppermute(pairs[step], ('depth', 'sample', 'filter'), links)  5.37 us
    ppermute x9, waiting for transfers between devices, across_samples(): lax.ppermute(field, 'sample', [(i, i ^ step) for i in range(count)])  4.91 us
    ppermute x6, starting transfers between devices, swap_filter(): return lax.ppermute(field, 'filter', [(0, 1), (1, 0)])  2.41 us
  transfers between devices with their start and end apart: 24, of which 6 were waited for; matrix products, arithmetic and copies ran while one was open for 1% of the time, Pallas kernels for 15%

profile of v2, /device:TPU:0, one launch (start us, length us, event | category | flops | bytes accessed | tf_op | source)
XLA Modules:
  0.0 66.7 jit_solution(116497464542744781)
XLA Ops:
  0.7 3.1 %collective-permute-start = (f32[2,8,8,128]{3,2,1,0:T(8,128)}, f32[2,8,8,128]{3,2,1,0:T(8,128)S(1)}, u32[]{:S(2)}, u32[]{:S(2)}) collective-permute-start(f32[2,8,8,128]{3,2,1,0:T(8,128)} %bitcast.18), channel_id=1, source_target_pairs={{0,8},{8,16},{16,24},{24,0},{1,9},{9,17},{17,25},{25,1},{2,10},{10... | collective-permute-start | bytes 196616 | tf_op jit(solution)/shard_map/ppermute | solution.py:410
  3.8 2.1 %collective-permute-start.1 = (f32[2,8,8,128]{3,2,1,0:T(8,128)}, f32[2,8,8,128]{3,2,1,0:T(8,128)S(1)}, u32[]{:S(2)}, u32[]{:S(2)}) collective-permute-start(f32[2,8,8,128]{3,2,1,0:T(8,128)} %bitcast.19), channel_id=1, source_target_pairs={{0,24},{8,0},{16,8},{24,16},{1,25},{9,1},{17,9},{25,17},{2,26},{10... | collective-permute-start | bytes 196616 | tf_op jit(solution)/shard_map/ppermute | solution.py:410
  5.8 0.9 %stage.1 = (f32[2,2,8,8,128]{4,3,2,1,0:T(8,128)S(1)}, f32[2,8,8,128]{3,2,1,0:T(8,128)S(1)}) custom-call(f32[2,8,8,128]{3,2,1,0:T(8,128)} %bitcast.16, f32[2,8,8,128]{3,2,1,0:T(8,128)} %bitcast.17, f32[2,8,8,128]{3,2,1,0:T(8,128)} %bitcast.20), custom_call_target="tpu_custom_call" | custom-call | tf_op jit(solution)/shard_map/stage/pallas_call | solution.py:257
  6.8 1.5 %collective-permute-done.before_ref.refs_1_ = f32[2,8,8,128]{3,2,1,0:T(8,128)S(1)} collective-permute-done((f32[2,8,8,128]{3,2,1,0:T(8,128)}, f32[2,8,8,128]{3,2,1,0:T(8,128)S(1)}, u32[]{:S(2)}, u32[]{:S(2)}) %collective-permute-start) | collective-permute-done | bytes 65568 | tf_op jit(solution)/shard_map/ppermute | solution.py:410
  8.3 0.6 collective-permute-done.1.after_ref.refs_3_
  8.9 3.3 %shard_map.76 = (f32[2,8,8,128]{3,2,1,0:T(8,128)S(1)}, f32[2,8,8,128]{3,2,1,0:T(8,128)S(1)}) custom-call(f32[2,8,8,128]{3,2,1,0:T(8,128)S(1)} %collective-permute-done.before_ref.refs_1_, f32[2,8,8,128]{3,2,1,0:T(8,128)S(1)} %get-tuple-element.13.own_ref.refs_0_, f32[2,8,8,128]{3,2,1,0:T(8,128)S(1)} %collective-permute-done.1.after_ref.refs_3_, ...), custom_call_target="tpu_custom_call" | custom-call | flops 679477248 | bytes 3538944 | tf_op jit(solution)/shard_map/pallas_call | solution.py:229
  12.3 0.1 collective-permute-start.2
  12.3 1.6 %collective-permute-start.10 = (f32[2,2,8,8,128]{4,3,2,1,0:T(8,128)S(1)}, f32[2,2,8,8,128]{4,3,2,1,0:T(8,128)S(1)}, u32[]{:S(2)}, u32[]{:S(2)}) collective-permute-start(f32[2,2,8,8,128]{4,3,2,1,0:T(8,128)S(1)} %get-tuple-element.16.refs_0_), channel_id=1, source_target_pairs={{0,2},{2,0},{4,6},{6,4},{1,3},{3,1},{5,7},{7,5},{8,10},{10,8},{12,... | collective-permute-start | bytes 393224 | tf_op jit(solution)/shard_map/ppermute | solution.py:418
  13.9 0.0 collective-permute-done.2
  13.9 1.2 %collective-permute-start.3 = (f32[2,8,8,128]{3,2,1,0:T(8,128)S(1)}, f32[2,8,8,128]{3,2,1,0:T(8,128)S(1)}, u32[]{:S(2)}, u32[]{:S(2)}) collective-permute-start(f32[2,8,8,128]{3,2,1,0:T(8,128)S(1)} %fusion.4.own_ref.refs_0_), channel_id=1, source_target_pairs={{0,8},{8,16},{16,24},{24,0},{1,9},{9,17},{17,25},{25,1},{2,10},{10... | collective-permute-start | bytes 196616 | tf_op jit(solution)/shard_map/ppermute | solution.py:410
  15.1 2.7 %collective-permute-start.4 = (f32[2,8,8,128]{3,2,1,0:T(8,128)S(1)}, f32[2,8,8,128]{3,2,1,0:T(8,128)S(1)}, u32[]{:S(2)}, u32[]{:S(2)}) collective-permute-start(f32[2,8,8,128]{3,2,1,0:T(8,128)S(1)} %fusion.4.own_ref.refs_0_), channel_id=1, source_target_pairs={{0,24},{8,0},{16,8},{24,16},{1,25},{9,1},{17,9},{25,17},{2,26},{10... | collective-permute-start | bytes 196616 | tf_op jit(solution)/shard_map/ppermute | solution.py:410
  17.8 1.5 %collective-permute-start.11 = (f32[2,2,8,8,128]{4,3,2,1,0:T(8,128)S(1)}, f32[2,2,8,8,128]{4,3,2,1,0:T(8,128)S(1)}, u32[]{:S(2)}, u32[]{:S(2)}) collective-permute-start(f32[2,2,8,8,128]{4,3,2,1,0:T(8,128)S(1)} %get-tuple-element.16.refs_0_), channel_id=1, source_target_pairs={{0,4},{2,6},{4,0},{6,2},{1,5},{3,7},{5,1},{7,3},{8,12},{10,14},{12... | collective-permute-start | bytes 393224 | tf_op jit(solution)/shard_map/ppermute | solution.py:418
  19.3 1.1 %collective-permute-start.12 = (f32[2,2,8,8,128]{4,3,2,1,0:T(8,128)S(1)}, f32[2,2,8,8,128]{4,3,2,1,0:T(8,128)S(1)}, u32[]{:S(2)}, u32[]{:S(2)}) collective-permute-start(f32[2,2,8,8,128]{4,3,2,1,0:T(8,128)S(1)} %get-tuple-element.16.refs_0_), channel_id=1, source_target_pairs={{0,6},{2,4},{4,2},{6,0},{1,7},{3,5},{5,3},{7,1},{8,14},{10,12},{12... | collective-permute-start | bytes 393224 | tf_op jit(solution)/shard_map/ppermute | solution.py:418
  20.5 0.1 collective-permute-start.20
  20.5 0.1 collective-permute-done.4.after_ref.refs_3_
  20.6 2.7 %collective-permute-start.6 = (f32[2,8,8,128]{3,2,1,0:T(8,128)S(1)}, f32[2,8,8,128]{3,2,1,0:T(8,128)S(1)}, u32[]{:S(2)}, u32[]{:S(2)}) collective-permute-start(f32[2,8,8,128]{3,2,1,0:T(8,128)S(1)} %fusion.4.own_ref.refs_0_), channel_id=1, source_target_pairs={{0,16},{8,24},{16,0},{24,8},{1,17},{9,25},{17,1},{25,9},{2,18},{10... | collective-permute-start | bytes 196616 | tf_op jit(solution)/shard_map/ppermute | solution.py:410
  23.4 2.1 %shard_map.77 = (f32[2,8,8,128]{3,2,1,0:T(8,128)S(1)}, f32[2,8,8,128]{3,2,1,0:T(8,128)S(1)}) custom-call(f32[2,8,8,128]{3,2,1,0:T(8,128)S(1)} %collective-permute-done.3.before_ref.refs_1_, f32[2,8,8,128]{3,2,1,0:T(8,128)S(1)} %fusion.4.own_ref.refs_0_, f32[2,8,8,128]{3,2,1,0:T(8,128)S(1)} %collective-permute-done.4.after_ref.refs_3_, ...), custom_call_target="tpu_custom_call" | custom-call | flops 679477248 | bytes 3538944 | tf_op jit(solution)/shard_map/pallas_call | solution.py:229
  25.5 0.1 collective-permute-start.5
  25.6 0.2 pair.1
  25.9 3.0 %collective-permute-start.13 = (f32[4,2,8,8,128]{4,3,2,1,0:T(8,128)S(1)}, f32[4,2,8,8,128]{4,3,2,1,0:T(8,128)S(1)}, u32[]{:S(2)}, u32[]{:S(2)}) collective-permute-start(f32[4,2,8,8,128]{4,3,2,1,0:T(8,128)S(1)} %get-tuple-element.20), channel_id=1, source_target_pairs={{0,8},{2,10},{4,12},{6,14},{9,17},{11,19},{13,21},{15,23},{17,25},... | collective-permute-start | bytes 786440 | tf_op jit(solution)/shard_map/ppermute | solution.py:432
  28.8 1.3 %collective-permute-start.14 = (f32[4,2,8,8,128]{4,3,2,1,0:T(8,128)S(1)}, f32[4,2,8,8,128]{4,3,2,1,0:T(8,128)S(1)}, u32[]{:S(2)}, u32[]{:S(2)}) collective-permute-start(f32[4,2,8,8,128]{4,3,2,1,0:T(8,128)S(1)} %get-tuple-element.21), channel_id=1, source_target_pairs={{1,17},{3,19},{5,21},{7,23},{9,25},{11,27},{13,29},{15,31},{16,0},... | collective-permute-start | bytes 786440 | tf_op jit(solution)/shard_map/ppermute | solution.py:432
  30.1 1.3 %collective-permute-start.15 = (f32[4,2,8,8,128]{4,3,2,1,0:T(8,128)S(1)}, f32[4,2,8,8,128]{4,3,2,1,0:T(8,128)S(1)}, u32[]{:S(2)}, u32[]{:S(2)}) collective-permute-start(f32[4,2,8,8,128]{4,3,2,1,0:T(8,128)S(1)} %get-tuple-element.22), channel_id=1, source_target_pairs={{1,25},{3,27},{5,29},{7,31},{8,0},{10,2},{12,4},{14,6},{16,8},{18,... | collective-permute-start | bytes 786440 | tf_op jit(solution)/shard_map/ppermute | solution.py:432
  31.5 1.7 %collective-permute-start.16 = (f32[4,2,8,8,128]{4,3,2,1,0:T(8,128)S(1)}, f32[4,2,8,8,128]{4,3,2,1,0:T(8,128)S(1)}, u32[]{:S(2)}, u32[]{:S(2)}) collective-permute-start(f32[4,2,8,8,128]{4,3,2,1,0:T(8,128)S(1)} %get-tuple-element.19.refs_4_), channel_id=1, source_target_pairs={{0,1},{1,0},{2,3},{3,2},{4,5},{5,4},{6,7},{7,6},{8,9},{9,8},{10,11... | collective-permute-start | bytes 786440 | tf_op jit(solution)/shard_map/ppermute | solution.py:437
  33.2 0.0 collective-permute-done.5
  33.2 0.9 %collective-permute-start.7 = (f32[8,8,8,128]{3,2,1,0:T(8,128)S(1)}, f32[8,8,8,128]{3,2,1,0:T(8,128)S(1)}, u32[]{:S(2)}, u32[]{:S(2)}) collective-permute-start(f32[8,8,8,128]{3,2,1,0:T(8,128)S(1)} %join_depth.2.refs_0_), channel_id=1, source_target_pairs={{0,2},{2,0},{4,6},{6,4},{1,3},{3,1},{5,7},{7,5},{8,10},{10,8},{12,... | collective-permute-start | bytes 786440 | tf_op jit(solution)/shard_map/ppermute | solution.py:418
  34.0 2.6 %collective-permute-done.13.refs_5_ = f32[4,2,8,8,128]{4,3,2,1,0:T(8,128)S(1)} collective-permute-done((f32[4,2,8,8,128]{4,3,2,1,0:T(8,128)S(1)}, f32[4,2,8,8,128]{4,3,2,1,0:T(8,128)S(1)}, u32[]{:S(2)}, u32[]{:S(2)}) %collective-permute-start.13) | collective-permute-done | bytes 262176 | tf_op jit(solution)/shard_map/ppermute | solution.py:432
  36.6 1.5 %collective-permute-start.8 = (f32[8,8,8,128]{3,2,1,0:T(8,128)S(1)}, f32[8,8,8,128]{3,2,1,0:T(8,128)S(1)}, u32[]{:S(2)}, u32[]{:S(2)}) collective-permute-start(f32[8,8,8,128]{3,2,1,0:T(8,128)S(1)} %join_depth.2.refs_0_), channel_id=1, source_target_pairs={{0,4},{2,6},{4,0},{6,2},{1,5},{3,7},{5,1},{7,3},{8,12},{10,14},{12... | collective-permute-start | bytes 786440 | tf_op jit(solution)/shard_map/ppermute | solution.py:418
  38.2 2.8 %collective-permute-done.14.refs_6_ = f32[4,2,8,8,128]{4,3,2,1,0:T(8,128)S(1)} collective-permute-done((f32[4,2,8,8,128]{4,3,2,1,0:T(8,128)S(1)}, f32[4,2,8,8,128]{4,3,2,1,0:T(8,128)S(1)}, u32[]{:S(2)}, u32[]{:S(2)}) %collective-permute-start.14) | collective-permute-done | bytes 262176 | tf_op jit(solution)/shard_map/ppermute | solution.py:432
  40.9 1.9 %collective-permute-start.9 = (f32[8,8,8,128]{3,2,1,0:T(8,128)S(1)}, f32[8,8,8,128]{3,2,1,0:T(8,128)S(1)}, u32[]{:S(2)}, u32[]{:S(2)}) collective-permute-start(f32[8,8,8,128]{3,2,1,0:T(8,128)S(1)} %join_depth.2.refs_0_), channel_id=1, source_target_pairs={{0,6},{2,4},{4,2},{6,0},{1,7},{3,5},{5,3},{7,1},{8,14},{10,12},{12... | collective-permute-start | bytes 786440 | tf_op jit(solution)/shard_map/ppermute | solution.py:418
  42.9 0.0 collective-permute-done.15.refs_7_
  42.9 0.0 collective-permute-start.17
  42.9 0.0 collective-permute-done.16.refs_8_
  42.9 0.5 collective-permute-start.18
  43.4 0.1 collective-permute-start.19
  43.5 0.6 add_bitcast_fusion
  44.1 4.9 %collective-permute-done.8.refs_2_ = f32[8,8,8,128]{3,2,1,0:T(8,128)S(1)} collective-permute-done((f32[8,8,8,128]{3,2,1,0:T(8,128)S(1)}, f32[8,8,8,128]{3,2,1,0:T(8,128)S(1)}, u32[]{:S(2)}, u32[]{:S(2)}) %collective-permute-start.8) | collective-permute-done | bytes 262176 | tf_op jit(solution)/shard_map/ppermute | solution.py:418
  49.0 0.0 collective-permute-start.21
  49.0 0.0 collective-permute-done.9.refs_3_
  49.0 2.9 %collective-permute-start.22 = (f32[8,8,8,128]{3,2,1,0:T(8,128)S(1)}, f32[8,8,8,128]{3,2,1,0:T(8,128)S(1)}, u32[]{:S(2)}, u32[]{:S(2)}) collective-permute-start(f32[8,8,8,128]{3,2,1,0:T(8,128)S(1)} %join_depth.3.refs_0_), channel_id=1, source_target_pairs={{0,4},{2,6},{4,0},{6,2},{1,5},{3,7},{5,1},{7,3},{8,12},{10,14},{12... | collective-permute-start | bytes 786440 | tf_op jit(solution)/shard_map/ppermute | solution.py:418
  51.9 0.0 collective-permute-done.17.refs_9_
  51.9 1.4 %collective-permute-start.23 = (f32[8,8,8,128]{3,2,1,0:T(8,128)S(1)}, f32[8,8,8,128]{3,2,1,0:T(8,128)S(1)}, u32[]{:S(2)}, u32[]{:S(2)}) collective-permute-start(f32[8,8,8,128]{3,2,1,0:T(8,128)S(1)} %join_depth.3.refs_0_), channel_id=1, source_target_pairs={{0,6},{2,4},{4,2},{6,0},{1,7},{3,5},{5,3},{7,1},{8,14},{10,12},{12... | collective-permute-start | bytes 786440 | tf_op jit(solution)/shard_map/ppermute | solution.py:418
  53.3 0.0 collective-permute-done.18.refs_10_
  53.3 0.0 collective-permute-done.19.refs_11_
  53.3 6.6 %first_weight.1 = f32[27,64,128]{2,1,0:T(8,128)} custom-call(f32[8,8,8,128]{3,2,1,0:T(8,128)S(1)} %join_depth.2.refs_0_, f32[8,8,8,128]{3,2,1,0:T(8,128)S(1)} %collective-permute-done.7.refs_1_, f32[8,8,8,128]{3,2,1,0:T(8,128)S(1)} %collective-permute-done.8.refs_2_, f32[8,8,8,128]{3,2,1,0:T(8,128)S(1)} %collective-permute-done.9.refs_3_, ...), custom_call_target="tpu_custom_call" | custom-call | flops 3623878656 | bytes 4194304 | tf_op jit(solution)/shard_map/first_weight/pallas_call | solution.py:388
  60.0 0.0 collective-permute-done.21.refs_1_
  60.0 0.0 collective-permute-done.22.refs_2_
  60.0 0.0 collective-permute-done.23.refs_3_
  60.0 6.7 %second_weight.1 = f32[27,64,128]{2,1,0:T(8,128)} custom-call(f32[8,8,8,128]{3,2,1,0:T(8,128)S(1)} %join_depth.3.refs_0_, f32[8,8,8,128]{3,2,1,0:T(8,128)S(1)} %collective-permute-done.21.refs_1_, f32[8,8,8,128]{3,2,1,0:T(8,128)S(1)} %collective-permute-done.22.refs_2_, f32[8,8,8,128]{3,2,1,0:T(8,128)S(1)} %collective-permute-done.23.refs_3_, ...), custom_call_target="tpu_custom_call" | custom-call | flops 3623878656 | bytes 4194304 | tf_op jit(solution)/shard_map/second_weight/pallas_call | solution.py:388
  (14 shorter events, 0.1 us)
Async XLA Ops:
  0.6 19.8 %copy-start.1 = (f32[1,2,8,8,128]{4,3,2,1,0:T(8,128)S(1)}, f32[1,2,8,8,128]{4,3,2,1,0:T(8,128)}, u32[]{:S(2)}) copy-start(f32[1,2,8,8,128]{4,3,2,1,0:T(8,128)} %param.7) | copy-start | bytes 196612
  0.6 22.7 %copy-start = (f32[27,256,128]{2,1,0:T(8,128)S(1)}, f32[27,256,128]{2,1,0:T(8,128)}, u32[]{:S(2)}) copy-start(f32[27,256,128]{2,1,0:T(8,128)} %weight_ref.3) | copy-start | bytes 10616836
  0.7 7.7 %collective-permute-start = (f32[2,8,8,128]{3,2,1,0:T(8,128)}, f32[2,8,8,128]{3,2,1,0:T(8,128)S(1)}, u32[]{:S(2)}, u32[]{:S(2)}) collective-permute-start(f32[2,8,8,128]{3,2,1,0:T(8,128)} %bitcast.18), channel_id=1, source_target_pairs={{0,8},{8,16},{16,24},{24,0},{1,9},{9,17},{17,25},{25,1},{2,10},{10... | collective-permute-start | bytes 196616 | tf_op jit(solution)/shard_map/ppermute | solution.py:410
  3.8 5.2 %collective-permute-start.1 = (f32[2,8,8,128]{3,2,1,0:T(8,128)}, f32[2,8,8,128]{3,2,1,0:T(8,128)S(1)}, u32[]{:S(2)}, u32[]{:S(2)}) collective-permute-start(f32[2,8,8,128]{3,2,1,0:T(8,128)} %bitcast.19), channel_id=1, source_target_pairs={{0,24},{8,0},{16,8},{24,16},{1,25},{9,1},{17,9},{25,17},{2,26},{10... | collective-permute-start | bytes 196616 | tf_op jit(solution)/shard_map/ppermute | solution.py:410
  12.3 1.6 %collective-permute-start.2 = (f32[2,8,8,128]{3,2,1,0:T(8,128)S(1)}, f32[2,8,8,128]{3,2,1,0:T(8,128)S(1)}, u32[]{:S(2)}, u32[]{:S(2)}) collective-permute-start(f32[2,8,8,128]{3,2,1,0:T(8,128)S(1)} %get-tuple-element.15), channel_id=1, source_target_pairs={{0,1},{1,0},{2,3},{3,2},{4,5},{5,4},{6,7},{7,6},{8,9},{9,8},{10,11... | collective-permute-start | bytes 196616 | tf_op jit(solution)/shard_map/ppermute | solution.py:437
  12.3 13.2 %collective-permute-start.10 = (f32[2,2,8,8,128]{4,3,2,1,0:T(8,128)S(1)}, f32[2,2,8,8,128]{4,3,2,1,0:T(8,128)S(1)}, u32[]{:S(2)}, u32[]{:S(2)}) collective-permute-start(f32[2,2,8,8,128]{4,3,2,1,0:T(8,128)S(1)} %get-tuple-element.16.refs_0_), channel_id=1, source_target_pairs={{0,2},{2,0},{4,6},{6,4},{1,3},{3,1},{5,7},{7,5},{8,10},{10,8},{12,... | collective-permute-start | bytes 393224 | tf_op jit(solution)/shard_map/ppermute | solution.py:418
  13.9 6.5 %collective-permute-start.3 = (f32[2,8,8,128]{3,2,1,0:T(8,128)S(1)}, f32[2,8,8,128]{3,2,1,0:T(8,128)S(1)}, u32[]{:S(2)}, u32[]{:S(2)}) collective-permute-start(f32[2,8,8,128]{3,2,1,0:T(8,128)S(1)} %fusion.4.own_ref.refs_0_), channel_id=1, source_target_pairs={{0,8},{8,16},{16,24},{24,0},{1,9},{9,17},{17,25},{25,1},{2,10},{10... | collective-permute-start | bytes 196616 | tf_op jit(solution)/shard_map/ppermute | solution.py:410
  15.1 5.5 %collective-permute-start.4 = (f32[2,8,8,128]{3,2,1,0:T(8,128)S(1)}, f32[2,8,8,128]{3,2,1,0:T(8,128)S(1)}, u32[]{:S(2)}, u32[]{:S(2)}) collective-permute-start(f32[2,8,8,128]{3,2,1,0:T(8,128)S(1)} %fusion.4.own_ref.refs_0_), channel_id=1, source_target_pairs={{0,24},{8,0},{16,8},{24,16},{1,25},{9,1},{17,9},{25,17},{2,26},{10... | collective-permute-start | bytes 196616 | tf_op jit(solution)/shard_map/ppermute | solution.py:410
  17.8 7.8 %collective-permute-start.11 = (f32[2,2,8,8,128]{4,3,2,1,0:T(8,128)S(1)}, f32[2,2,8,8,128]{4,3,2,1,0:T(8,128)S(1)}, u32[]{:S(2)}, u32[]{:S(2)}) collective-permute-start(f32[2,2,8,8,128]{4,3,2,1,0:T(8,128)S(1)} %get-tuple-element.16.refs_0_), channel_id=1, source_target_pairs={{0,4},{2,6},{4,0},{6,2},{1,5},{3,7},{5,1},{7,3},{8,12},{10,14},{12... | collective-permute-start | bytes 393224 | tf_op jit(solution)/shard_map/ppermute | solution.py:418
  19.3 6.3 %collective-permute-start.12 = (f32[2,2,8,8,128]{4,3,2,1,0:T(8,128)S(1)}, f32[2,2,8,8,128]{4,3,2,1,0:T(8,128)S(1)}, u32[]{:S(2)}, u32[]{:S(2)}) collective-permute-start(f32[2,2,8,8,128]{4,3,2,1,0:T(8,128)S(1)} %get-tuple-element.16.refs_0_), channel_id=1, source_target_pairs={{0,6},{2,4},{4,2},{6,0},{1,7},{3,5},{5,3},{7,1},{8,14},{10,12},{12... | collective-permute-start | bytes 393224 | tf_op jit(solution)/shard_map/ppermute | solution.py:418
  20.5 11.0 %collective-permute-start.20 = (f32[2,8,8,128]{3,2,1,0:T(8,128)S(1)}, f32[2,8,8,128]{3,2,1,0:T(8,128)S(1)}, u32[]{:S(2)}, u32[]{:S(2)}) collective-permute-start(f32[2,8,8,128]{3,2,1,0:T(8,128)S(1)} %bitcast.21), channel_id=1, source_target_pairs={{0,16},{8,24},{16,0},{24,8},{1,17},{9,25},{17,1},{25,9},{2,18},{10... | collective-permute-start | bytes 196616 | tf_op jit(solution)/shard_map/ppermute | solution.py:410
  20.6 9.5 %collective-permute-start.6 = (f32[2,8,8,128]{3,2,1,0:T(8,128)S(1)}, f32[2,8,8,128]{3,2,1,0:T(8,128)S(1)}, u32[]{:S(2)}, u32[]{:S(2)}) collective-permute-start(f32[2,8,8,128]{3,2,1,0:T(8,128)S(1)} %fusion.4.own_ref.refs_0_), channel_id=1, source_target_pairs={{0,16},{8,24},{16,0},{24,8},{1,17},{9,25},{17,1},{25,9},{2,18},{10... | collective-permute-start | bytes 196616 | tf_op jit(solution)/shard_map/ppermute | solution.py:410
  25.5 7.6 %collective-permute-start.5 = (f32[2,8,8,128]{3,2,1,0:T(8,128)S(1)}, f32[2,8,8,128]{3,2,1,0:T(8,128)S(1)}, u32[]{:S(2)}, u32[]{:S(2)}) collective-permute-start(f32[2,8,8,128]{3,2,1,0:T(8,128)S(1)} %get-tuple-element.18), channel_id=1, source_target_pairs={{0,1},{1,0},{2,3},{3,2},{4,5},{5,4},{6,7},{7,6},{8,9},{9,8},{10,11... | collective-permute-start | bytes 196616 | tf_op jit(solution)/shard_map/ppermute | solution.py:437
  25.9 10.8 %collective-permute-start.13 = (f32[4,2,8,8,128]{4,3,2,1,0:T(8,128)S(1)}, f32[4,2,8,8,128]{4,3,2,1,0:T(8,128)S(1)}, u32[]{:S(2)}, u32[]{:S(2)}) collective-permute-start(f32[4,2,8,8,128]{4,3,2,1,0:T(8,128)S(1)} %get-tuple-element.20), channel_id=1, source_target_pairs={{0,8},{2,10},{4,12},{6,14},{9,17},{11,19},{13,21},{15,23},{17,25},... | collective-permute-start | bytes 786440 | tf_op jit(solution)/shard_map/ppermute | solution.py:432
  28.8 12.1 %collective-permute-start.14 = (f32[4,2,8,8,128]{4,3,2,1,0:T(8,128)S(1)}, f32[4,2,8,8,128]{4,3,2,1,0:T(8,128)S(1)}, u32[]{:S(2)}, u32[]{:S(2)}) collective-permute-start(f32[4,2,8,8,128]{4,3,2,1,0:T(8,128)S(1)} %get-tuple-element.21), channel_id=1, source_target_pairs={{1,17},{3,19},{5,21},{7,23},{9,25},{11,27},{13,29},{15,31},{16,0},... | collective-permute-start | bytes 786440 | tf_op jit(solution)/shard_map/ppermute | solution.py:432
  30.1 12.7 %collective-permute-start.15 = (f32[4,2,8,8,128]{4,3,2,1,0:T(8,128)S(1)}, f32[4,2,8,8,128]{4,3,2,1,0:T(8,128)S(1)}, u32[]{:S(2)}, u32[]{:S(2)}) collective-permute-start(f32[4,2,8,8,128]{4,3,2,1,0:T(8,128)S(1)} %get-tuple-element.22), channel_id=1, source_target_pairs={{1,25},{3,27},{5,29},{7,31},{8,0},{10,2},{12,4},{14,6},{16,8},{18,... | collective-permute-start | bytes 786440 | tf_op jit(solution)/shard_map/ppermute | solution.py:432
  31.5 11.4 %collective-permute-start.16 = (f32[4,2,8,8,128]{4,3,2,1,0:T(8,128)S(1)}, f32[4,2,8,8,128]{4,3,2,1,0:T(8,128)S(1)}, u32[]{:S(2)}, u32[]{:S(2)}) collective-permute-start(f32[4,2,8,8,128]{4,3,2,1,0:T(8,128)S(1)} %get-tuple-element.19.refs_4_), channel_id=1, source_target_pairs={{0,1},{1,0},{2,3},{3,2},{4,5},{5,4},{6,7},{7,6},{8,9},{9,8},{10,11... | collective-permute-start | bytes 786440 | tf_op jit(solution)/shard_map/ppermute | solution.py:437
  33.2 10.2 %collective-permute-start.7 = (f32[8,8,8,128]{3,2,1,0:T(8,128)S(1)}, f32[8,8,8,128]{3,2,1,0:T(8,128)S(1)}, u32[]{:S(2)}, u32[]{:S(2)}) collective-permute-start(f32[8,8,8,128]{3,2,1,0:T(8,128)S(1)} %join_depth.2.refs_0_), channel_id=1, source_target_pairs={{0,2},{2,0},{4,6},{6,4},{1,3},{3,1},{5,7},{7,5},{8,10},{10,8},{12,... | collective-permute-start | bytes 786440 | tf_op jit(solution)/shard_map/ppermute | solution.py:418
  36.6 12.4 %collective-permute-start.8 = (f32[8,8,8,128]{3,2,1,0:T(8,128)S(1)}, f32[8,8,8,128]{3,2,1,0:T(8,128)S(1)}, u32[]{:S(2)}, u32[]{:S(2)}) collective-permute-start(f32[8,8,8,128]{3,2,1,0:T(8,128)S(1)} %join_depth.2.refs_0_), channel_id=1, source_target_pairs={{0,4},{2,6},{4,0},{6,2},{1,5},{3,7},{5,1},{7,3},{8,12},{10,14},{12... | collective-permute-start | bytes 786440 | tf_op jit(solution)/shard_map/ppermute | solution.py:418
  40.9 8.1 %collective-permute-start.9 = (f32[8,8,8,128]{3,2,1,0:T(8,128)S(1)}, f32[8,8,8,128]{3,2,1,0:T(8,128)S(1)}, u32[]{:S(2)}, u32[]{:S(2)}) collective-permute-start(f32[8,8,8,128]{3,2,1,0:T(8,128)S(1)} %join_depth.2.refs_0_), channel_id=1, source_target_pairs={{0,6},{2,4},{4,2},{6,0},{1,7},{3,5},{5,3},{7,1},{8,14},{10,12},{12... | collective-permute-start | bytes 786440 | tf_op jit(solution)/shard_map/ppermute | solution.py:418
  42.9 9.0 %collective-permute-start.17 = (f32[4,2,8,8,128]{4,3,2,1,0:T(8,128)S(1)}, f32[4,2,8,8,128]{4,3,2,1,0:T(8,128)S(1)}, u32[]{:S(2)}, u32[]{:S(2)}) collective-permute-start(f32[4,2,8,8,128]{4,3,2,1,0:T(8,128)S(1)} %collective-permute-done.13.refs_5_), channel_id=1, source_target_pairs={{0,1},{1,0},{2,3},{3,2},{4,5},{5,4},{6,7},{7,6},{8,9},{9,8},{10,11... | collective-permute-start | bytes 786440 | tf_op jit(solution)/shard_map/ppermute | solution.py:437
  42.9 10.5 %collective-permute-start.18 = (f32[4,2,8,8,128]{4,3,2,1,0:T(8,128)S(1)}, f32[4,2,8,8,128]{4,3,2,1,0:T(8,128)S(1)}, u32[]{:S(2)}, u32[]{:S(2)}) collective-permute-start(f32[4,2,8,8,128]{4,3,2,1,0:T(8,128)S(1)} %collective-permute-done.14.refs_6_), channel_id=1, source_target_pairs={{0,1},{1,0},{2,3},{3,2},{4,5},{5,4},{6,7},{7,6},{8,9},{9,8},{10,11... | collective-permute-start | bytes 786440 | tf_op jit(solution)/shard_map/ppermute | solution.py:437
  43.4 9.9 %collective-permute-start.19 = (f32[4,2,8,8,128]{4,3,2,1,0:T(8,128)S(1)}, f32[4,2,8,8,128]{4,3,2,1,0:T(8,128)S(1)}, u32[]{:S(2)}, u32[]{:S(2)}) collective-permute-start(f32[4,2,8,8,128]{4,3,2,1,0:T(8,128)S(1)} %collective-permute-done.15.refs_7_), channel_id=1, source_target_pairs={{0,1},{1,0},{2,3},{3,2},{4,5},{5,4},{6,7},{7,6},{8,9},{9,8},{10,11... | collective-permute-start | bytes 786440 | tf_op jit(solution)/shard_map/ppermute | solution.py:437
  49.0 11.0 %collective-permute-start.21 = (f32[8,8,8,128]{3,2,1,0:T(8,128)S(1)}, f32[8,8,8,128]{3,2,1,0:T(8,128)S(1)}, u32[]{:S(2)}, u32[]{:S(2)}) collective-permute-start(f32[8,8,8,128]{3,2,1,0:T(8,128)S(1)} %join_depth.3.refs_0_), channel_id=1, source_target_pairs={{0,2},{2,0},{4,6},{6,4},{1,3},{3,1},{5,7},{7,5},{8,10},{10,8},{12,... | collective-permute-start | bytes 786440 | tf_op jit(solution)/shard_map/ppermute | solution.py:418
  49.0 11.0 %collective-permute-start.22 = (f32[8,8,8,128]{3,2,1,0:T(8,128)S(1)}, f32[8,8,8,128]{3,2,1,0:T(8,128)S(1)}, u32[]{:S(2)}, u32[]{:S(2)}) collective-permute-start(f32[8,8,8,128]{3,2,1,0:T(8,128)S(1)} %join_depth.3.refs_0_), channel_id=1, source_target_pairs={{0,4},{2,6},{4,0},{6,2},{1,5},{3,7},{5,1},{7,3},{8,12},{10,14},{12... | collective-permute-start | bytes 786440 | tf_op jit(solution)/shard_map/ppermute | solution.py:418
  51.9 8.1 %collective-permute-start.23 = (f32[8,8,8,128]{3,2,1,0:T(8,128)S(1)}, f32[8,8,8,128]{3,2,1,0:T(8,128)S(1)}, u32[]{:S(2)}, u32[]{:S(2)}) collective-permute-start(f32[8,8,8,128]{3,2,1,0:T(8,128)S(1)} %join_depth.3.refs_0_), channel_id=1, source_target_pairs={{0,6},{2,4},{4,2},{6,0},{1,7},{3,5},{5,3},{7,1},{8,14},{10,12},{12... | collective-permute-start | bytes 786440 | tf_op jit(solution)/shard_map/ppermute | solution.py:418

commit v3 on v2

--- a/solution.py
+++ b/solution.py
@@ -92,7 +92,7 @@
         and breadth == 8
         and height % 2 == 0
         and second_weight.shape[1] == halves * lanes
-        and 2 * second_weight.shape[1] == depths * lanes
+        and depths == 2 * halves
         and samples & (samples - 1) == 0
         and rows * lanes * 4 <= 2**21
     )
@@ -210,10 +210,6 @@
     split_halves(total_ref[...].T, keep_ref, send_ref)
 
 
-def full_spec(shape):
-    return pl.BlockSpec(shape, lambda *_: (0,) * len(shape))
-
-
 def spread_scratch(planes, height, breadth, lanes, parts):
     return [
         pltpu.VMEM((3, parts, planes, height // 2 + 1, 2 * breadth, lanes), jnp.bfloat16),
@@ -290,8 +286,9 @@
 
 def pair_kernel(count, *refs):
     fields, outs = refs[:count], refs[count:]
-    depths = len(outs)
     place = lax.axis_index("depth")
+    inside = place // 2 == lax.axis_index("filter")
+    targets = (place, place ^ jnp.where(inside, 1, 2), place ^ 3)
     lanes = fields[0].shape[-1]
     half = lanes // 2
     for sample in range(count):
@@ -301,79 +298,81 @@
         lane = lax.broadcasted_iota(jnp.int32, first.shape, 1)
         low = jnp.where(lane < half, first, pltpu.roll(activated, half, axis=1)).reshape(shape)
         high = jnp.where(lane < half, pltpu.roll(first, half, axis=1), activated).reshape(shape)
-        for step in range(depths):
-            lower = lax.rem(place + step, 2) == 0
-            outs[step][sample] = jnp.where(lower, low, high)
+        for out, target in zip(outs, targets):
+            out[sample] = jnp.where(target % 2 == 0, low, high)
 
 
 def pair_call(fields):
-    depths, count = lax.axis_size("depth"), len(fields)
-    shape = (count, *fields[0].shape[1:])
+    shape = (len(fields), *fields[0].shape[1:])
     return pl.pallas_call(
-        functools.partial(pair_kernel, count),
-        out_shape=[jax.ShapeDtypeStruct(shape, jnp.float32)] * depths,
+        functools.partial(pair_kernel, len(fields)),
+        out_shape=[jax.ShapeDtypeStruct(shape, jnp.float32)] * 3,
         compiler_params=pltpu.CompilerParams(vmem_limit_bytes=6 * 2**20),
         name="pair",
     )(*fields)
 
 
 def weight_kernel(count, second, factor, *refs):
-    out_ref, even_ref, odd_ref, grad_ref = refs[-4:]
-    fields, pairs = refs[:count], refs[count:-4]
+    out_ref, even_ref, odd_ref, grad_ref, done_ref, semaphores = refs[-6:]
+    fields, pairs = refs[:count], refs[count:-6]
     depths = len(pairs) // 2
     near, far = pairs[:depths], pairs[depths:]
-    step = pl.program_id(0)
     planes, height, breadth, lanes = fields[0].shape
     share = planes // depths
     half = lanes // 2
     rows = planes * height * breadth
 
-    @pl.when(step == 0)
-    def _():
-        place = lax.axis_index("depth")
-        owner = place // 2 == lax.axis_index("filter")
-        for sample in range(count):
-            for ref in (even_ref, odd_ref):
-                for tap in range(3):
-                    for plane in (0, planes + 1):
-                        ref[tap, sample, plane] = jnp.zeros(ref.shape[3:], ref.dtype)
-            for hop, index in itertools.product(range(depths), range(share)):
-                plane = lax.rem(place + depths - hop, depths) * share + index
-                cells = jnp.where(owner, near[hop][sample, index], far[hop][sample, index])
-                lane = lax.broadcasted_iota(jnp.int32, cells.shape, 2)
-                swapped = pltpu.roll(cells, half, axis=2)
-                lower = lane < half
-                cells = jnp.where(lower, swapped, cells) if second else jnp.where(lower, cells, swapped)
-                high = cells.astype(jnp.bfloat16).astype(jnp.float32)
-                cells = jnp.where(lower, high, cells - high)
-                for tap in range(3):
-                    even, odd = row_pairs(column_shift(cells, tap))
-                    even_ref[tap, sample, plane + 1] = even.astype(jnp.bfloat16)
-                    odd_ref[tap, sample, plane + 1] = odd.astype(jnp.bfloat16)
-            turned = fields[sample][...].reshape(rows, lanes).T
-            for part, value in enumerate(two_parts(turned)):
-                grad_ref[part * lanes : (part + 1) * lanes, sample * rows : (sample + 1) * rows] = value
-
-    def cell(row_tap, column_tap):
+    place = lax.axis_index("depth")
+    owner = place // 2 == lax.axis_index("filter")
+    for sample in range(count):
+        for ref in (even_ref, odd_ref):
+            for tap in range(3):
+                for plane in (0, planes + 1):
+                    ref[tap, sample, plane] = jnp.zeros(ref.shape[3:], ref.dtype)
+        for hop, index in itertools.product(range(depths), range(share)):
+            plane = (place ^ hop) * share + index
+            cells = jnp.where(owner, near[hop][sample, index], far[hop][sample, index])
+            lane = lax.broadcasted_iota(jnp.int32, cells.shape, 2)
+            swapped = pltpu.roll(cells, half, axis=2)
+            lower = lane < half
+            cells = jnp.where(lower, swapped, cells) if second else jnp.where(lower, cells, swapped)
+            high = cells.astype(jnp.bfloat16).astype(jnp.float32)
+            cells = jnp.where(lower, high, cells - high)
+            for tap in range(3):
+                even, odd = row_pairs(column_shift(cells, tap))
+                even_ref[tap, sample, plane + 1] = even.astype(jnp.bfloat16)
+                odd_ref[tap, sample, plane + 1] = odd.astype(jnp.bfloat16)
+        turned = fields[sample][...].reshape(rows, lanes).T
+        for part, value in enumerate(two_parts(turned)):
+            grad_ref[part * lanes : (part + 1) * lanes, sample * rows : (sample + 1) * rows] = value
+
+    def cell(depth_tap, row_tap, column_tap):
         return jnp.concatenate(
             [
-                slab(even_ref, odd_ref, (column_tap, sample), step, planes, row_tap)
+                slab(even_ref, odd_ref, (column_tap, sample), depth_tap, planes, row_tap)
                 for sample in range(count)
             ],
             axis=0,
         )
 
-    taps = [(row_tap, column_tap) for row_tap in range(3) for column_tap in range(3)]
-    for start in range(0, 9, 2):
-        group = taps[start : start + 2]
-        right = [cell(*tap) for tap in group]
-        right = jnp.concatenate(right, axis=1) if len(right) > 1 else right[0]
+    def deliver(third):
+        where = pl.ds(9 * third, 9)
+        return pltpu.make_async_copy(done_ref.at[where], out_ref.at[where], semaphores.at[third])
+
+    taps = list(itertools.product(range(3), repeat=3))
+    for start in range(0, 27, 4):
+        group = taps[start : start + 4]
+        right = jnp.concatenate([cell(*tap) for tap in group], axis=1)
         product = jnp.dot(grad_ref[...], right, preferred_element_type=jnp.float32)
         product = product[:lanes] + product[lanes:]
         for index in range(len(group)):
             piece = product[:, index * lanes : (index + 1) * lanes]
             piece = piece + pltpu.roll(piece, half, axis=1)
-            out_ref[start + index] = piece.T[:half] * factor
+            done_ref[start + index] = piece.T[:half] * factor
+            if (start + index) % 9 == 8:
+                deliver((start + index) // 9).start()
+    for third in range(3):
+        deliver(third).wait()
 
 
 def weight_call(fields, near, far, second, factor):
@@ -384,12 +383,13 @@
         pltpu.VMEM((3, count, planes + 2, height // 2 + 1, 2 * breadth, lanes), jnp.bfloat16),
         pltpu.VMEM((3, count, planes + 2, height // 2, 2 * breadth, lanes), jnp.bfloat16),
         pltpu.VMEM((2 * lanes, count * rows), jnp.bfloat16),
+        pltpu.VMEM((27, lanes // 2, lanes), jnp.float32),
+        pltpu.SemaphoreType.DMA((3,)),
     ]
     return pl.pallas_call(
         functools.partial(weight_kernel, count, second, factor),
-        grid=(3,),
-        in_specs=[full_spec(each.shape) for each in (*fields, *near, *far)],
-        out_specs=pl.BlockSpec((9, lanes // 2, lanes), lambda step: (step, 0, 0)),
+        in_specs=[pl.BlockSpec(memory_space=pltpu.VMEM)] * (len(fields) + 2 * len(near)),
+        out_specs=pl.BlockSpec(memory_space=pltpu.HBM),
         out_shape=jax.ShapeDtypeStruct((27, lanes // 2, lanes), jnp.float32),
         scratch_shapes=scratch,
         compiler_params=pltpu.CompilerParams(vmem_limit_bytes=20 * 2**20),
@@ -419,18 +419,25 @@
     return moved
 
 
-def owners_around_depth(pairs):
+def pairs_around_depth(pairs):
     depths, samples, halves = axis_sizes()
-    moved = [pairs[0]]
-    for step in range(1, depths):
-        links = []
-        for depth, sample in itertools.product(range(depths), range(samples)):
-            target = (depth + step) % depths
-            half = target // 2
-            place = lambda value: (value * samples + sample) * halves + half
-            links.append((place(depth), place(target)))
-        moved.append(lax.ppermute(pairs[step], ("depth", "sample", "filter"), links))
-    return moved
+    place = lambda depth, sample, half: (depth * samples + sample) * halves + half
+    links = [], []
+    for depth, sample, half in itertools.product(range(depths), range(samples), range(halves)):
+        source = place(depth, sample, half)
+        if depth // 2 == half:
+            links[0].append((source, place(depth ^ 1, sample, half)))
+        else:
+            links[0].append((source, place(depth ^ 2, sample, 1 - half)))
+            links[1].append((source, place(depth ^ 3, sample, half)))
+    own, *moved = pairs
+    for index in range(2):
+        axes = ("depth", "sample", "filter")
+        moved[index] = lax.ppermute(moved[index], axes, links[index])
+    swapped = [swap_filter(piece) for piece in (own, *moved)]
+    near = [own, moved[0], swapped[1], moved[1]]
+    far = [swapped[0], swapped[1], moved[0], swapped[2]]
+    return near, far
 
 
 def swap_filter(field):
@@ -450,8 +457,7 @@
     all_grads = across_samples(grads)
     pre_grads = around_depth(pre_grad)
     pairs = pair_call(fields)
-    near = owners_around_depth(pairs)
-    far = [swap_filter(piece) for piece in near]
+    near, far = pairs_around_depth(pairs)
     all_pre = across_samples(join_depth(pre_grads))
     keep, send = back_call(pre_grads[1], pre_grads[0], pre_grads[-1], first_weight, False)
     input_grad = (keep + swap_filter(send)).reshape(local_shape)

time: 66.9 us -> 71.4 us (1.067)
  waiting for transfers between devices: 12.5 us -> 18.3 us
  Pallas kernels: 20 us -> 17.9 us
  starting transfers between devices: 32.7 us -> 33.5 us
    ppermute x6, waiting for transfers between devices: 2.24 us -> 9.44 us  [around_depth(): moved[step] = lax.ppermute(field, 'depth', links)]
    ppermute x3 -> x2, waiting for transfers between devices: 5.37 us -> 0.01 us  [pairs_around_depth(): moved[index] = lax.ppermute(moved[index], axes, links[index])]
    ppermute x6, starting transfers between devices: 11.9 us -> 16.7 us  [around_depth(): moved[step] = lax.ppermute(field, 'depth', links)]
    ppermute x3 -> x2, starting transfers between devices: 5.55 us -> 1.36 us  [pairs_around_depth(): moved[index] = lax.ppermute(moved[index], axes, links[index])]
    ppermute x9, waiting for transfers between devices: 4.91 us -> 8.87 us  [across_samples(): lax.ppermute(field, 'sample', [(i, i ^ step) for i in range(count)])]
    pallas_call x3, Pallas kernels: 13.5 us -> 11.4 us  [the longest x2 11.2 us: weight_call(): pl.pallas_call(functools.partial(weight_kernel, count, second, factor), i...]
    ppermute x6 -> x5, starting transfers between devices: 2.41 us -> 3.9 us  [swap_filter(): return lax.ppermute(field, 'filter', [(0, 1), (1, 0)])]
    ppermute x9, starting transfers between devices: 12.8 us -> 11.6 us  [across_samples(): lax.ppermute(field, 'sample', [(i, i ^ step) for i in range(count)])]
  transfers between devices with their start and end apart: 24 -> 22, of which waited for: 6 -> 7; matrix products, arithmetic and copies ran while one was open for 1% -> 1% of each run, Pallas kernels for 15% -> 17%
where the time goes in v3:
time: 71.4 us; the launch traced here: 71.2 us
  starting transfers between devices  33.5 us (47%)
  waiting for transfers between devices  18.3 us (26%)
  Pallas kernels  17.9 us (25%)
  between operations  0.77 us (1%)
    ppermute x6, starting transfers between devices, around_depth(): moved[step] = lax.ppermute(field, 'depth', links)  16.7 us
    ppermute x9, starting transfers between devices, across_samples(): lax.ppermute(field, 'sample', [(i, i ^ step) for i in range(count)])  11.6 us
    pallas_call x2, Pallas kernels, weight_call(): pl.pallas_call(functools.partial(weight_kernel, count, second, factor), i...  11.2 us
    ppermute x6, waiting for transfers between devices, around_depth(): moved[step] = lax.ppermute(field, 'depth', links)  9.44 us
    ppermute x9, waiting for transfers between devices, across_samples(): lax.ppermute(field, 'sample', [(i, i ^ step) for i in range(count)])  8.87 us
    pallas_call x2, Pallas kernels, back_call(): pl.pallas_call(back_kernel, in_specs=[pl.BlockSpec(memory_space=pltpu.VME...  5.48 us
    ppermute x5, starting transfers between devices, swap_filter(): return lax.ppermute(field, 'filter', [(0, 1), (1, 0)])  3.9 us
  transfers between devices with their start and end apart: 22, of which 7 were waited for; matrix products, arithmetic and copies ran while one was open for 1% of the time, Pallas kernels for 17%

profile of v3, /device:TPU:0, one launch (start us, length us, event | category | flops | bytes accessed | tf_op | source)
XLA Modules:
  0.0 71.2 jit_solution(17726910013664196061)
XLA Ops:
  0.7 5.1 %collective-permute-start.1 = (f32[2,8,8,128]{3,2,1,0:T(8,128)}, f32[2,8,8,128]{3,2,1,0:T(8,128)S(1)}, u32[]{:S(2)}, u32[]{:S(2)}) collective-permute-start(f32[2,8,8,128]{3,2,1,0:T(8,128)} %bitcast.18), channel_id=1, source_target_pairs={{0,24},{8,0},{16,8},{24,16},{1,25},{9,1},{17,9},{25,17},{2,26},{10... | collective-permute-start | bytes 196616 | tf_op jit(solution)/shard_map/ppermute | solution.py:410
  5.8 0.0 collective-permute-start
  5.8 0.9 %stage.1 = (f32[2,2,8,8,128]{4,3,2,1,0:T(8,128)S(1)}, f32[2,8,8,128]{3,2,1,0:T(8,128)S(1)}) custom-call(f32[2,8,8,128]{3,2,1,0:T(8,128)} %bitcast.16, f32[2,8,8,128]{3,2,1,0:T(8,128)} %bitcast.17, f32[2,8,8,128]{3,2,1,0:T(8,128)} %bitcast.20), custom_call_target="tpu_custom_call" | custom-call | tf_op jit(solution)/shard_map/stage/pallas_call | solution.py:253
  6.7 2.5 %collective-permute-start.12 = (f32[2,2,8,8,128]{4,3,2,1,0:T(8,128)S(1)}, f32[2,2,8,8,128]{4,3,2,1,0:T(8,128)S(1)}, u32[]{:S(2)}, u32[]{:S(2)}) collective-permute-start(f32[2,2,8,8,128]{4,3,2,1,0:T(8,128)S(1)} %get-tuple-element.15.refs_0_), channel_id=1, source_target_pairs={{0,6},{2,4},{4,2},{6,0},{1,7},{3,5},{5,3},{7,1},{8,14},{10,12},{12... | collective-permute-start | bytes 393224 | tf_op jit(solution)/shard_map/ppermute | solution.py:418
  9.2 0.5 collective-permute-start.11
  9.7 0.5 collective-permute-start.10
  10.3 0.0 collective-permute-done.1.after_ref.refs_3_
  10.3 1.8 %collective-permute-done.before_ref.refs_1_ = f32[2,8,8,128]{3,2,1,0:T(8,128)S(1)} collective-permute-done((f32[2,8,8,128]{3,2,1,0:T(8,128)}, f32[2,8,8,128]{3,2,1,0:T(8,128)S(1)}, u32[]{:S(2)}, u32[]{:S(2)}) %collective-permute-start) | collective-permute-done | bytes 65568 | tf_op jit(solution)/shard_map/ppermute | solution.py:410
  12.1 3.3 %shard_map.76 = (f32[2,8,8,128]{3,2,1,0:T(8,128)S(1)}, f32[2,8,8,128]{3,2,1,0:T(8,128)S(1)}) custom-call(f32[2,8,8,128]{3,2,1,0:T(8,128)S(1)} %collective-permute-done.before_ref.refs_1_, f32[2,8,8,128]{3,2,1,0:T(8,128)S(1)} %get-tuple-element.12.own_ref.refs_0_, f32[2,8,8,128]{3,2,1,0:T(8,128)S(1)} %collective-permute-done.1.after_ref.refs_3_, ...), custom_call_target="tpu_custom_call" | custom-call | flops 679477248 | bytes 3538944 | tf_op jit(solution)/shard_map/pallas_call | solution.py:225
  15.4 0.1 collective-permute-start.2
  15.5 0.0 collective-permute-done.12.refs_3_
  15.5 0.0 collective-permute-done.11.refs_2_
  15.5 0.0 collective-permute-done.10.refs_1_
  15.5 0.2 pair.1
  15.7 0.1 collective-permute-start.13
  15.8 1.3 %collective-permute-start.15 = (f32[4,2,8,8,128]{4,3,2,1,0:T(8,128)S(1)}, f32[4,2,8,8,128]{4,3,2,1,0:T(8,128)S(1)}, u32[]{:S(2)}, u32[]{:S(2)}) collective-permute-start(f32[4,2,8,8,128]{4,3,2,1,0:T(8,128)S(1)} %get-tuple-element.20), channel_id=1, source_target_pairs={{1,25},{3,27},{5,29},{7,31},{9,17},{11,19},{13,21},{15,23},{16,8},... | collective-permute-start | bytes 786440 | tf_op jit(solution)/shard_map/ppermute | solution.py:436
  17.1 3.3 %collective-permute-start.16 = (f32[4,2,8,8,128]{4,3,2,1,0:T(8,128)S(1)}, f32[4,2,8,8,128]{4,3,2,1,0:T(8,128)S(1)}, u32[]{:S(2)}, u32[]{:S(2)}) collective-permute-start(f32[4,2,8,8,128]{4,3,2,1,0:T(8,128)S(1)} %get-tuple-element.18.refs_4_), channel_id=1, source_target_pairs={{0,1},{1,0},{2,3},{3,2},{4,5},{5,4},{6,7},{7,6},{8,9},{9,8},{10,11... | collective-permute-start | bytes 786440 | tf_op jit(solution)/shard_map/ppermute | solution.py:444
  20.4 0.0 collective-permute-done.2
  20.5 1.3 %collective-permute-start.4 = (f32[2,8,8,128]{3,2,1,0:T(8,128)S(1)}, f32[2,8,8,128]{3,2,1,0:T(8,128)S(1)}, u32[]{:S(2)}, u32[]{:S(2)}) collective-permute-start(f32[2,8,8,128]{3,2,1,0:T(8,128)S(1)} %fusion.4.own_ref.refs_0_), channel_id=1, source_target_pairs={{0,24},{8,0},{16,8},{24,16},{1,25},{9,1},{17,9},{25,17},{2,26},{10... | collective-permute-start | bytes 196616 | tf_op jit(solution)/shard_map/ppermute | solution.py:410
  21.8 0.8 %collective-permute-start.3 = (f32[2,8,8,128]{3,2,1,0:T(8,128)S(1)}, f32[2,8,8,128]{3,2,1,0:T(8,128)S(1)}, u32[]{:S(2)}, u32[]{:S(2)}) collective-permute-start(f32[2,8,8,128]{3,2,1,0:T(8,128)S(1)} %fusion.4.own_ref.refs_0_), channel_id=1, source_target_pairs={{0,8},{8,16},{16,24},{24,0},{1,9},{9,17},{17,25},{25,1},{2,10},{10... | collective-permute-start | bytes 196616 | tf_op jit(solution)/shard_map/ppermute | solution.py:410
  22.6 3.4 %collective-permute-done.4.after_ref.refs_3_ = f32[2,8,8,128]{3,2,1,0:T(8,128)S(1)} collective-permute-done((f32[2,8,8,128]{3,2,1,0:T(8,128)S(1)}, f32[2,8,8,128]{3,2,1,0:T(8,128)S(1)}, u32[]{:S(2)}, u32[]{:S(2)}) %collective-permute-start.4) | collective-permute-done | bytes 65568 | tf_op jit(solution)/shard_map/ppermute | solution.py:410
  25.9 9.4 %collective-permute-start.6 = (f32[2,8,8,128]{3,2,1,0:T(8,128)S(1)}, f32[2,8,8,128]{3,2,1,0:T(8,128)S(1)}, u32[]{:S(2)}, u32[]{:S(2)}) collective-permute-start(f32[2,8,8,128]{3,2,1,0:T(8,128)S(1)} %fusion.4.own_ref.refs_0_), channel_id=1, source_target_pairs={{0,16},{8,24},{16,0},{24,8},{1,17},{9,25},{17,1},{25,9},{2,18},{10... | collective-permute-start | bytes 196616 | tf_op jit(solution)/shard_map/ppermute | solution.py:410
  35.3 0.0 collective-permute-done.3.before_ref.refs_1_
  35.3 0.1 collective-permute-start.18
  35.4 2.2 %shard_map.77 = (f32[2,8,8,128]{3,2,1,0:T(8,128)S(1)}, f32[2,8,8,128]{3,2,1,0:T(8,128)S(1)}) custom-call(f32[2,8,8,128]{3,2,1,0:T(8,128)S(1)} %collective-permute-done.3.before_ref.refs_1_, f32[2,8,8,128]{3,2,1,0:T(8,128)S(1)} %fusion.4.own_ref.refs_0_, f32[2,8,8,128]{3,2,1,0:T(8,128)S(1)} %collective-permute-done.4.after_ref.refs_3_, ...), custom_call_target="tpu_custom_call" | custom-call | flops 679477248 | bytes 3538944 | tf_op jit(solution)/shard_map/pallas_call | solution.py:225
  37.6 1.4 %collective-permute-done.6.refs_2_ = f32[2,8,8,128]{3,2,1,0:T(8,128)S(1)} collective-permute-done((f32[2,8,8,128]{3,2,1,0:T(8,128)S(1)}, f32[2,8,8,128]{3,2,1,0:T(8,128)S(1)}, u32[]{:S(2)}, u32[]{:S(2)}) %collective-permute-start.6) | collective-permute-done | bytes 65568 | tf_op jit(solution)/shard_map/ppermute | solution.py:410
  38.9 0.0 collective-permute-start.5
  39.0 2.9 %collective-permute-done.18.refs_2_ = f32[2,8,8,128]{3,2,1,0:T(8,128)S(1)} collective-permute-done((f32[2,8,8,128]{3,2,1,0:T(8,128)S(1)}, f32[2,8,8,128]{3,2,1,0:T(8,128)S(1)}, u32[]{:S(2)}, u32[]{:S(2)}) %collective-permute-start.18) | collective-permute-done | bytes 65568 | tf_op jit(solution)/shard_map/ppermute | solution.py:410
  41.9 2.4 %collective-permute-start.9 = (f32[8,8,8,128]{3,2,1,0:T(8,128)S(1)}, f32[8,8,8,128]{3,2,1,0:T(8,128)S(1)}, u32[]{:S(2)}, u32[]{:S(2)}) collective-permute-start(f32[8,8,8,128]{3,2,1,0:T(8,128)S(1)} %join_depth.2.refs_0_), channel_id=1, source_target_pairs={{0,6},{2,4},{4,2},{6,0},{1,7},{3,5},{5,3},{7,1},{8,14},{10,12},{12... | collective-permute-start | bytes 786440 | tf_op jit(solution)/shard_map/ppermute | solution.py:418
  44.2 0.0 collective-permute-done.5
  44.2 0.6 collective-permute-start.8
  44.8 0.0 collective-permute-done.13.refs_5_.refs_10_
  44.8 0.5 collective-permute-start.7
  45.4 0.0 collective-permute-done.15.refs_7_
  45.4 0.0 collective-permute-start.14
  45.4 0.5 collective-permute-start.17
  45.9 0.6 add_bitcast_fusion
  46.6 5.4 %collective-permute-done.9.refs_3_ = f32[8,8,8,128]{3,2,1,0:T(8,128)S(1)} collective-permute-done((f32[8,8,8,128]{3,2,1,0:T(8,128)S(1)}, f32[8,8,8,128]{3,2,1,0:T(8,128)S(1)}, u32[]{:S(2)}, u32[]{:S(2)}) %collective-permute-start.9) | collective-permute-done | bytes 262176 | tf_op jit(solution)/shard_map/ppermute | solution.py:418
  52.0 2.2 %collective-permute-start.21 = (f32[8,8,8,128]{3,2,1,0:T(8,128)S(1)}, f32[8,8,8,128]{3,2,1,0:T(8,128)S(1)}, u32[]{:S(2)}, u32[]{:S(2)}) collective-permute-start(f32[8,8,8,128]{3,2,1,0:T(8,128)S(1)} %join_depth.3.refs_0_), channel_id=1, source_target_pairs={{0,6},{2,4},{4,2},{6,0},{1,7},{3,5},{5,3},{7,1},{8,14},{10,12},{12... | collective-permute-start | bytes 786440 | tf_op jit(solution)/shard_map/ppermute | solution.py:418
  54.2 2.9 %collective-permute-done.8.refs_2_ = f32[8,8,8,128]{3,2,1,0:T(8,128)S(1)} collective-permute-done((f32[8,8,8,128]{3,2,1,0:T(8,128)S(1)}, f32[8,8,8,128]{3,2,1,0:T(8,128)S(1)}, u32[]{:S(2)}, u32[]{:S(2)}) %collective-permute-start.8) | collective-permute-done | bytes 262176 | tf_op jit(solution)/shard_map/ppermute | solution.py:418
  57.1 1.4 %collective-permute-start.20 = (f32[8,8,8,128]{3,2,1,0:T(8,128)S(1)}, f32[8,8,8,128]{3,2,1,0:T(8,128)S(1)}, u32[]{:S(2)}, u32[]{:S(2)}) collective-permute-start(f32[8,8,8,128]{3,2,1,0:T(8,128)S(1)} %join_depth.3.refs_0_), channel_id=1, source_target_pairs={{0,4},{2,6},{4,0},{6,2},{1,5},{3,7},{5,1},{7,3},{8,12},{10,14},{12... | collective-permute-start | bytes 786440 | tf_op jit(solution)/shard_map/ppermute | solution.py:418
  58.5 0.0 collective-permute-done.7.refs_1_
  58.5 0.9 %collective-permute-start.19 = (f32[8,8,8,128]{3,2,1,0:T(8,128)S(1)}, f32[8,8,8,128]{3,2,1,0:T(8,128)S(1)}, u32[]{:S(2)}, u32[]{:S(2)}) collective-permute-start(f32[8,8,8,128]{3,2,1,0:T(8,128)S(1)} %join_depth.3.refs_0_), channel_id=1, source_target_pairs={{0,2},{2,0},{4,6},{6,4},{1,3},{3,1},{5,7},{7,5},{8,10},{10,8},{12,... | collective-permute-start | bytes 786440 | tf_op jit(solution)/shard_map/ppermute | solution.py:418
  59.4 5.6 %first_weight.1 = f32[27,64,128]{2,1,0:T(8,128)} custom-call(f32[8,8,8,128]{3,2,1,0:T(8,128)S(1)} %join_depth.2.refs_0_, f32[8,8,8,128]{3,2,1,0:T(8,128)S(1)} %collective-permute-done.7.refs_1_, f32[8,8,8,128]{3,2,1,0:T(8,128)S(1)} %collective-permute-done.8.refs_2_, f32[8,8,8,128]{3,2,1,0:T(8,128)S(1)} %collective-permute-done.9.refs_3_, ...), custom_call_target="tpu_custom_call" | custom-call | flops 3623878656 | bytes 4194304 | tf_op jit(solution)/shard_map/first_weight/pallas_call | solution.py:389
  65.0 0.0 collective-permute-done.21.refs_3_
  65.1 0.5 collective-permute-done.20.refs_2_
  65.6 0.0 collective-permute-done.19.refs_1_
  65.6 5.6 %second_weight.1 = f32[27,64,128]{2,1,0:T(8,128)} custom-call(f32[8,8,8,128]{3,2,1,0:T(8,128)S(1)} %join_depth.3.refs_0_, f32[8,8,8,128]{3,2,1,0:T(8,128)S(1)} %collective-permute-done.19.refs_1_, f32[8,8,8,128]{3,2,1,0:T(8,128)S(1)} %collective-permute-done.20.refs_2_, f32[8,8,8,128]{3,2,1,0:T(8,128)S(1)} %collective-permute-done.21.refs_3_, ...), custom_call_target="tpu_custom_call" | custom-call | flops 3623878656 | bytes 4194304 | tf_op jit(solution)/shard_map/second_weight/pallas_call | solution.py:389
  (10 shorter events, 0.1 us)
Async XLA Ops:
  0.6 34.7 %copy-start.1 = (f32[1,2,8,8,128]{4,3,2,1,0:T(8,128)S(1)}, f32[1,2,8,8,128]{4,3,2,1,0:T(8,128)}, u32[]{:S(2)}) copy-start(f32[1,2,8,8,128]{4,3,2,1,0:T(8,128)} %param.7) | copy-start | bytes 196612
  0.6 34.7 %copy-start = (f32[27,256,128]{2,1,0:T(8,128)S(1)}, f32[27,256,128]{2,1,0:T(8,128)}, u32[]{:S(2)}) copy-start(f32[27,256,128]{2,1,0:T(8,128)} %weight_ref.3) | copy-start | bytes 10616836
  0.7 9.6 %collective-permute-start.1 = (f32[2,8,8,128]{3,2,1,0:T(8,128)}, f32[2,8,8,128]{3,2,1,0:T(8,128)S(1)}, u32[]{:S(2)}, u32[]{:S(2)}) collective-permute-start(f32[2,8,8,128]{3,2,1,0:T(8,128)} %bitcast.18), channel_id=1, source_target_pairs={{0,24},{8,0},{16,8},{24,16},{1,25},{9,1},{17,9},{25,17},{2,26},{10... | collective-permute-start | bytes 196616 | tf_op jit(solution)/shard_map/ppermute | solution.py:410
  5.8 6.3 %collective-permute-start = (f32[2,8,8,128]{3,2,1,0:T(8,128)}, f32[2,8,8,128]{3,2,1,0:T(8,128)S(1)}, u32[]{:S(2)}, u32[]{:S(2)}) collective-permute-start(f32[2,8,8,128]{3,2,1,0:T(8,128)} %bitcast.19), channel_id=1, source_target_pairs={{0,8},{8,16},{16,24},{24,0},{1,9},{9,17},{17,25},{25,1},{2,10},{10... | collective-permute-start | bytes 196616 | tf_op jit(solution)/shard_map/ppermute | solution.py:410
  6.7 8.7 %collective-permute-start.12 = (f32[2,2,8,8,128]{4,3,2,1,0:T(8,128)S(1)}, f32[2,2,8,8,128]{4,3,2,1,0:T(8,128)S(1)}, u32[]{:S(2)}, u32[]{:S(2)}) collective-permute-start(f32[2,2,8,8,128]{4,3,2,1,0:T(8,128)S(1)} %get-tuple-element.15.refs_0_), channel_id=1, source_target_pairs={{0,6},{2,4},{4,2},{6,0},{1,7},{3,5},{5,3},{7,1},{8,14},{10,12},{12... | collective-permute-start | bytes 393224 | tf_op jit(solution)/shard_map/ppermute | solution.py:418
  9.2 6.2 %collective-permute-start.11 = (f32[2,2,8,8,128]{4,3,2,1,0:T(8,128)S(1)}, f32[2,2,8,8,128]{4,3,2,1,0:T(8,128)S(1)}, u32[]{:S(2)}, u32[]{:S(2)}) collective-permute-start(f32[2,2,8,8,128]{4,3,2,1,0:T(8,128)S(1)} %get-tuple-element.15.refs_0_), channel_id=1, source_target_pairs={{0,4},{2,6},{4,0},{6,2},{1,5},{3,7},{5,1},{7,3},{8,12},{10,14},{12... | collective-permute-start | bytes 393224 | tf_op jit(solution)/shard_map/ppermute | solution.py:418
  9.7 5.8 %collective-permute-start.10 = (f32[2,2,8,8,128]{4,3,2,1,0:T(8,128)S(1)}, f32[2,2,8,8,128]{4,3,2,1,0:T(8,128)S(1)}, u32[]{:S(2)}, u32[]{:S(2)}) collective-permute-start(f32[2,2,8,8,128]{4,3,2,1,0:T(8,128)S(1)} %get-tuple-element.15.refs_0_), channel_id=1, source_target_pairs={{0,2},{2,0},{4,6},{6,4},{1,3},{3,1},{5,7},{7,5},{8,10},{10,8},{12,... | collective-permute-start | bytes 393224 | tf_op jit(solution)/shard_map/ppermute | solution.py:418
  15.4 5.1 %collective-permute-start.2 = (f32[2,8,8,128]{3,2,1,0:T(8,128)S(1)}, f32[2,8,8,128]{3,2,1,0:T(8,128)S(1)}, u32[]{:S(2)}, u32[]{:S(2)}) collective-permute-start(f32[2,8,8,128]{3,2,1,0:T(8,128)S(1)} %get-tuple-element.14), channel_id=1, source_target_pairs={{0,1},{1,0},{2,3},{3,2},{4,5},{5,4},{6,7},{7,6},{8,9},{9,8},{10,11... | collective-permute-start | bytes 196616 | tf_op jit(solution)/shard_map/ppermute | solution.py:444
  15.7 29.1 %collective-permute-start.13 = (f32[4,2,8,8,128]{4,3,2,1,0:T(8,128)S(1)}, f32[4,2,8,8,128]{4,3,2,1,0:T(8,128)S(1)}, u32[]{:S(2)}, u32[]{:S(2)}) collective-permute-start(f32[4,2,8,8,128]{4,3,2,1,0:T(8,128)S(1)} %get-tuple-element.19), channel_id=1, source_target_pairs={{0,8},{1,16},{2,10},{3,18},{4,12},{5,20},{6,14},{7,22},{8,0},{9,24... | collective-permute-start | bytes 786440 | tf_op jit(solution)/shard_map/ppermute | solution.py:436
  15.8 29.6 %collective-permute-start.15 = (f32[4,2,8,8,128]{4,3,2,1,0:T(8,128)S(1)}, f32[4,2,8,8,128]{4,3,2,1,0:T(8,128)S(1)}, u32[]{:S(2)}, u32[]{:S(2)}) collective-permute-start(f32[4,2,8,8,128]{4,3,2,1,0:T(8,128)S(1)} %get-tuple-element.20), channel_id=1, source_target_pairs={{1,25},{3,27},{5,29},{7,31},{9,17},{11,19},{13,21},{15,23},{16,8},... | collective-permute-start | bytes 786440 | tf_op jit(solution)/shard_map/ppermute | solution.py:436
  17.1 28.3 %collective-permute-start.16 = (f32[4,2,8,8,128]{4,3,2,1,0:T(8,128)S(1)}, f32[4,2,8,8,128]{4,3,2,1,0:T(8,128)S(1)}, u32[]{:S(2)}, u32[]{:S(2)}) collective-permute-start(f32[4,2,8,8,128]{4,3,2,1,0:T(8,128)S(1)} %get-tuple-element.18.refs_4_), channel_id=1, source_target_pairs={{0,1},{1,0},{2,3},{3,2},{4,5},{5,4},{6,7},{7,6},{8,9},{9,8},{10,11... | collective-permute-start | bytes 786440 | tf_op jit(solution)/shard_map/ppermute | solution.py:444
  20.5 5.5 %collective-permute-start.4 = (f32[2,8,8,128]{3,2,1,0:T(8,128)S(1)}, f32[2,8,8,128]{3,2,1,0:T(8,128)S(1)}, u32[]{:S(2)}, u32[]{:S(2)}) collective-permute-start(f32[2,8,8,128]{3,2,1,0:T(8,128)S(1)} %fusion.4.own_ref.refs_0_), channel_id=1, source_target_pairs={{0,24},{8,0},{16,8},{24,16},{1,25},{9,1},{17,9},{25,17},{2,26},{10... | collective-permute-start | bytes 196616 | tf_op jit(solution)/shard_map/ppermute | solution.py:410
  21.8 13.6 %collective-permute-start.3 = (f32[2,8,8,128]{3,2,1,0:T(8,128)S(1)}, f32[2,8,8,128]{3,2,1,0:T(8,128)S(1)}, u32[]{:S(2)}, u32[]{:S(2)}) collective-permute-start(f32[2,8,8,128]{3,2,1,0:T(8,128)S(1)} %fusion.4.own_ref.refs_0_), channel_id=1, source_target_pairs={{0,8},{8,16},{16,24},{24,0},{1,9},{9,17},{17,25},{25,1},{2,10},{10... | collective-permute-start | bytes 196616 | tf_op jit(solution)/shard_map/ppermute | solution.py:410
  25.9 13.0 %collective-permute-start.6 = (f32[2,8,8,128]{3,2,1,0:T(8,128)S(1)}, f32[2,8,8,128]{3,2,1,0:T(8,128)S(1)}, u32[]{:S(2)}, u32[]{:S(2)}) collective-permute-start(f32[2,8,8,128]{3,2,1,0:T(8,128)S(1)} %fusion.4.own_ref.refs_0_), channel_id=1, source_target_pairs={{0,16},{8,24},{16,0},{24,8},{1,17},{9,25},{17,1},{25,9},{2,18},{10... | collective-permute-start | bytes 196616 | tf_op jit(solution)/shard_map/ppermute | solution.py:410
  35.3 6.6 %collective-permute-start.18 = (f32[2,8,8,128]{3,2,1,0:T(8,128)S(1)}, f32[2,8,8,128]{3,2,1,0:T(8,128)S(1)}, u32[]{:S(2)}, u32[]{:S(2)}) collective-permute-start(f32[2,8,8,128]{3,2,1,0:T(8,128)S(1)} %bitcast.21), channel_id=1, source_target_pairs={{0,16},{8,24},{16,0},{24,8},{1,17},{9,25},{17,1},{25,9},{2,18},{10... | collective-permute-start | bytes 196616 | tf_op jit(solution)/shard_map/ppermute | solution.py:410
  38.9 5.3 %collective-permute-start.5 = (f32[2,8,8,128]{3,2,1,0:T(8,128)S(1)}, f32[2,8,8,128]{3,2,1,0:T(8,128)S(1)}, u32[]{:S(2)}, u32[]{:S(2)}) collective-permute-start(f32[2,8,8,128]{3,2,1,0:T(8,128)S(1)} %get-tuple-element.17), channel_id=1, source_target_pairs={{0,1},{1,0},{2,3},{3,2},{4,5},{5,4},{6,7},{7,6},{8,9},{9,8},{10,11... | collective-permute-start | bytes 196616 | tf_op jit(solution)/shard_map/ppermute | solution.py:444
  41.9 10.1 %collective-permute-start.9 = (f32[8,8,8,128]{3,2,1,0:T(8,128)S(1)}, f32[8,8,8,128]{3,2,1,0:T(8,128)S(1)}, u32[]{:S(2)}, u32[]{:S(2)}) collective-permute-start(f32[8,8,8,128]{3,2,1,0:T(8,128)S(1)} %join_depth.2.refs_0_), channel_id=1, source_target_pairs={{0,6},{2,4},{4,2},{6,0},{1,7},{3,5},{5,3},{7,1},{8,14},{10,12},{12... | collective-permute-start | bytes 786440 | tf_op jit(solution)/shard_map/ppermute | solution.py:418
  44.2 12.8 %collective-permute-start.8 = (f32[8,8,8,128]{3,2,1,0:T(8,128)S(1)}, f32[8,8,8,128]{3,2,1,0:T(8,128)S(1)}, u32[]{:S(2)}, u32[]{:S(2)}) collective-permute-start(f32[8,8,8,128]{3,2,1,0:T(8,128)S(1)} %join_depth.2.refs_0_), channel_id=1, source_target_pairs={{0,4},{2,6},{4,0},{6,2},{1,5},{3,7},{5,1},{7,3},{8,12},{10,14},{12... | collective-permute-start | bytes 786440 | tf_op jit(solution)/shard_map/ppermute | solution.py:418
  44.8 13.7 %collective-permute-start.7 = (f32[8,8,8,128]{3,2,1,0:T(8,128)S(1)}, f32[8,8,8,128]{3,2,1,0:T(8,128)S(1)}, u32[]{:S(2)}, u32[]{:S(2)}) collective-permute-start(f32[8,8,8,128]{3,2,1,0:T(8,128)S(1)} %join_depth.2.refs_0_), channel_id=1, source_target_pairs={{0,2},{2,0},{4,6},{6,4},{1,3},{3,1},{5,7},{7,5},{8,10},{10,8},{12,... | collective-permute-start | bytes 786440 | tf_op jit(solution)/shard_map/ppermute | solution.py:418
  45.4 14.0 %collective-permute-start.14 = (f32[4,2,8,8,128]{4,3,2,1,0:T(8,128)S(1)}, f32[4,2,8,8,128]{4,3,2,1,0:T(8,128)S(1)}, u32[]{:S(2)}, u32[]{:S(2)}) collective-permute-start(f32[4,2,8,8,128]{4,3,2,1,0:T(8,128)S(1)} %collective-permute-done.13.refs_5_.refs_10_), channel_id=1, source_target_pairs={{0,1},{1,0},{2,3},{3,2},{4,5},{5,4},{6,7},{7,6},{8,9},{9,8},{10,11... | collective-permute-start | bytes 786440 | tf_op jit(solution)/shard_map/ppermute | solution.py:444
  45.4 14.0 %collective-permute-start.17 = (f32[4,2,8,8,128]{4,3,2,1,0:T(8,128)S(1)}, f32[4,2,8,8,128]{4,3,2,1,0:T(8,128)S(1)}, u32[]{:S(2)}, u32[]{:S(2)}) collective-permute-start(f32[4,2,8,8,128]{4,3,2,1,0:T(8,128)S(1)} %collective-permute-done.15.refs_7_), channel_id=1, source_target_pairs={{0,1},{1,0},{2,3},{3,2},{4,5},{5,4},{6,7},{7,6},{8,9},{9,8},{10,11... | collective-permute-start | bytes 786440 | tf_op jit(solution)/shard_map/ppermute | solution.py:444
  52.0 13.1 %collective-permute-start.21 = (f32[8,8,8,128]{3,2,1,0:T(8,128)S(1)}, f32[8,8,8,128]{3,2,1,0:T(8,128)S(1)}, u32[]{:S(2)}, u32[]{:S(2)}) collective-permute-start(f32[8,8,8,128]{3,2,1,0:T(8,128)S(1)} %join_depth.3.refs_0_), channel_id=1, source_target_pairs={{0,6},{2,4},{4,2},{6,0},{1,7},{3,5},{5,3},{7,1},{8,14},{10,12},{12... | collective-permute-start | bytes 786440 | tf_op jit(solution)/shard_map/ppermute | solution.py:418
  57.1 8.5 %collective-permute-start.20 = (f32[8,8,8,128]{3,2,1,0:T(8,128)S(1)}, f32[8,8,8,128]{3,2,1,0:T(8,128)S(1)}, u32[]{:S(2)}, u32[]{:S(2)}) collective-permute-start(f32[8,8,8,128]{3,2,1,0:T(8,128)S(1)} %join_depth.3.refs_0_), channel_id=1, source_target_pairs={{0,4},{2,6},{4,0},{6,2},{1,5},{3,7},{5,1},{7,3},{8,12},{10,14},{12... | collective-permute-start | bytes 786440 | tf_op jit(solution)/shard_map/ppermute | solution.py:418
  58.5 7.0 %collective-permute-start.19 = (f32[8,8,8,128]{3,2,1,0:T(8,128)S(1)}, f32[8,8,8,128]{3,2,1,0:T(8,128)S(1)}, u32[]{:S(2)}, u32[]{:S(2)}) collective-permute-start(f32[8,8,8,128]{3,2,1,0:T(8,128)S(1)} %join_depth.3.refs_0_), channel_id=1, source_target_pairs={{0,2},{2,0},{4,6},{6,4},{1,3},{3,1},{5,7},{7,5},{8,10},{10,8},{12,... | collective-permute-start | bytes 786440 | tf_op jit(solution)/shard_map/ppermute | solution.py:418
